TPU v7x, 512 devices: a whole 4x8x8 slice. The times are simulated.
512 devices in a mesh: seq: 64 (over y, x, core), chan: 8 (over z).
Axes of the slice: x: 4, y: 8, z: 8, core: 2. Of those that a mesh axis runs over, the one named last changes fastest.
Arguments:
- x_in: bfloat16 [131072, 2048], P('seq', 'chan'), may hold values from -6 to 6
- gate_in: bfloat16 [131072, 2048], P('seq', 'chan'), may hold values from -70 to 70
- b_in: bfloat16 [131072, 64], P('seq'), may hold values from -0.75 to 0.75
- c_in: bfloat16 [131072, 64], P('seq'), may hold values from -6 to 6
- step_size: float32 [32, 131072], P('chan', 'seq'), may hold values from 0 to 1, as said below
- log_keep: float32 [32, 131072], P('chan', 'seq'), may hold values from -2 to 0
- skip_gain: float32 [32], P('chan'), may hold values from 0.5 to 1.5
- norm_gain: float32 [2048], P('chan'), may hold values from 0.25 to 1.75
Outputs:
- mixed: bfloat16 [131072, 2048], P('seq', 'chan')
Inputs may be any that keep to these rules, and one draw needn't show every extreme that they name: `step_size`: positive.
All inputs are finite; a program needn't handle non-finite values.
Results may differ from a plain program's by a relative error of at most 0.005.
Values sent between devices are 32-bit elements; how exact they have to be, the bound alone decides.
A program may use at most 64 MiB of HBM per device.

v0:
```python
import jax
import jax.numpy as jnp
from jax import lax
from jax.sharding import Mesh
from jax.sharding import PartitionSpec as P

CH = 2048
BLOCK = 256
SEQ = ("seq_0", "seq_1", "seq_2")


epsilon = 1e-05


def nothing_yet(shard, identity):
    return jax.tree.map(
        lambda part, zero: jnp.zeros_like(part) + jnp.asarray(zero, part.dtype), shard, identity
    )


def all_in_one(shard, axis):
    leaves = jax.tree.leaves(shard)
    order = sorted(range(len(leaves)), key=lambda k: -leaves[k].size)
    width = (1, *leaves[order[0]].shape)[-1]
    lines = [
        jnp.pad(leaves[k].reshape(-1), (0, -leaves[k].size % width)).reshape(-1, width)
        for k in order
    ]
    both, at, found = (lax.all_gather(jnp.concatenate(lines), axis), 0, {})
    for k, line in zip(order, lines):
        piece = both[:, at : at + len(line)].reshape(len(both), -1)
        found[k] = piece[:, : leaves[k].size].reshape(-1, *leaves[k].shape)
        at += len(line)
    numbers = iter(range(len(leaves)))
    return jax.tree.map(lambda _: found[next(numbers)], shard)


def prefix_by_axis(shard, axes, combine, identity):
    before = start = nothing_yet(shard, identity)
    total = shard
    for axis in reversed(axes):
        length, here = (lax.axis_size(axis), lax.axis_index(axis))
        pieces = all_in_one(total, axis)
        inside, total = (start, start)
        for k in range(length):
            passed = k < here
            total = combine(total, jax.tree.map(lambda part: part[k], pieces))
            inside = jax.tree.map(lambda new, old: jnp.where(passed, new, old), total, inside)
        before = combine(inside, before)
    return before


def copy_for_each(shard, axis):
    length = lax.axis_size(axis)
    return lax.all_to_all(
        jnp.broadcast_to(shard[None], (length, *shard.shape)), axis, 0, 0, tiled=True
    )


def of_everyone(shard, axis):
    return copy_for_each(shard, axis).sum(axis=0)


def compose(earlier, later_pair):
    early_total, early_state = earlier
    late_total, late_state = later_pair
    return (early_total + late_total, jnp.exp(late_total)[:, None] * early_state + late_state)


def incoming_state(device_total, end_flat):
    head_count, flat_size = end_flat.shape
    zeros_pair = (
        jnp.zeros((head_count,), jnp.float32),
        jnp.zeros((head_count, flat_size), jnp.float32),
    )
    _, entering = prefix_by_axis((device_total, end_flat), SEQ, compose, zeros_pair)
    return entering


def apply_state(c_blocks, cum_keep, states):
    state_high = states.astype(jnp.bfloat16)
    state_low = (states - state_high.astype(jnp.float32)).astype(jnp.bfloat16)
    projected = jnp.einsum(
        "btn,bhpn->bthp", c_blocks, state_high, preferred_element_type=jnp.float32
    )
    projected = projected + jnp.einsum(
        "btn,bhpn->bthp", c_blocks, state_low, preferred_element_type=jnp.float32
    )
    return jnp.exp(cum_keep).transpose(1, 2, 0)[:, :, :, None] * projected


def per_device(x_in, gate_in, b_in, c_in, step_size, log_keep, skip_gain, norm_gain):
    tokens, channels = x_in.shape
    head_count = step_size.shape[0]
    head_width = channels // head_count
    nstate = b_in.shape[1]
    block_count = tokens // BLOCK
    x_blocks = x_in.reshape(block_count, BLOCK, head_count, head_width)
    b_blocks = b_in.reshape(block_count, BLOCK, nstate)
    c_blocks = c_in.reshape(block_count, BLOCK, nstate)
    step_blocks = step_size.reshape(head_count, block_count, BLOCK)
    cum_keep = jnp.cumsum(log_keep.reshape(head_count, block_count, BLOCK), axis=2)
    block_total = cum_keep[:, :, -1]
    decayed_b = (
        (jnp.exp(block_total[:, :, None] - cum_keep) * step_blocks)[:, :, :, None]
        * b_blocks[None].astype(jnp.float32)
    ).astype(jnp.bfloat16)
    block_state = jnp.einsum(
        "bshp,hbsn->bhpn", x_blocks, decayed_b, preferred_element_type=jnp.float32
    )

    def carry_blocks(running, block_input):
        total_now, state_now = block_input
        return (jnp.exp(total_now)[:, None, None] * running + state_now, running)

    end_state, starts = lax.scan(
        carry_blocks,
        jnp.zeros((head_count, head_width, nstate), jnp.float32),
        (block_total.T, block_state),
    )
    device_total = jnp.sum(block_total, axis=1)
    prefix_total = jnp.cumsum(block_total, axis=1) - block_total
    end_flat = end_state.reshape(head_count, head_width * nstate)
    scores = jnp.einsum("btn,bsn->bts", c_blocks, b_blocks, preferred_element_type=jnp.float32)
    row_index = lax.broadcasted_iota(jnp.int32, (BLOCK, BLOCK), 0)
    col_index = lax.broadcasted_iota(jnp.int32, (BLOCK, BLOCK), 1)
    causal = (row_index >= col_index)[None, None]
    log_gaps = cum_keep[:, :, :, None] - cum_keep[:, :, None, :]
    decays = jnp.where(causal, jnp.exp(jnp.where(causal, log_gaps, 0.0)), 0.0)
    weights = (scores[None] * decays * step_blocks[:, :, None, :]).astype(jnp.bfloat16)
    output = jnp.einsum(
        "hbts,bshp->bthp", weights, x_blocks, preferred_element_type=jnp.float32
    ) + apply_state(c_blocks, cum_keep, starts)
    entering = incoming_state(device_total, end_flat).reshape(head_count, head_width, nstate)
    spread_state = jnp.broadcast_to(entering[None], (block_count, head_count, head_width, nstate))
    output = output + apply_state(c_blocks, cum_keep + prefix_total[:, :, None], spread_state)
    output = output + skip_gain[None, None, :, None] * x_blocks.astype(jnp.float32)
    output = output.reshape(tokens, channels)
    gated_out = output * jax.nn.silu(gate_in.astype(jnp.float32))
    squares = jnp.sum(gated_out * gated_out, axis=1)
    summed = of_everyone(squares, "chan")
    row_factor = lax.rsqrt(summed / CH + epsilon)
    return (gated_out * row_factor[:, None] * norm_gain[None, :]).astype(jnp.bfloat16)


def solution(mesh):
    split = Mesh(
        mesh.devices.reshape(8, 4, 2, mesh.shape["chan"]), ("seq_0", "seq_1", "seq_2", "chan")
    )
    placed = (
        P(SEQ, "chan"),
        P(SEQ, "chan"),
        P(SEQ, None),
        P(SEQ, None),
        P("chan", SEQ),
        P("chan", SEQ),
        P("chan"),
        P("chan"),
    )
    return jax.shard_map(
        per_device, mesh=split, in_specs=placed, out_specs=P(SEQ, "chan"), check_vma=False
    )
```

profile of v0, /device:TPU:2, one launch (start us, length us, event | category | flops | bytes accessed | tf_op | source)
XLA Modules:
  0.0 119.7 jit_solution(18137246634973519460)
XLA Ops:
  0.8 2.3 %reduce-window.6 = f32[4,8,2,128]{3,1,2,0:T(8,128)S(1)} reduce-window(f32[4,8,2,128]{3,1,2,0:T(8,128)S(1)} %copy.139, f32[]{:T(128)} %constant.23.clone.1), window={size=1x1x1x128 pad=0_0x0_0x0_0x127_0}, to_apply=%region_0.0 | reduce-window | flops 1040384 | bytes 65540 | tf_op jit(solution)/shard_map/reduce-window
  4.3 1.5 %exponential_bitcast_fusion = (f32[8,256,4]{1,0,2:T(8,128)}, f32[4,8,256]{2,1,0:T(8,128)S(1)}) fusion(f32[4,8,256]{2,1,0:T(8,128)S(1)} %get-tuple-element.97, f32[4,8]{1,0:T(4,128)S(1)} %get-tuple-element.83, f32[1,4,8,256]{3,1,2,0:T(4,128)} %bitcast.180, f32[4,8]{1,0:T(4,128)S(1)} %get-tuple-element.84), kind=kLoop, calls=%fused_computation.70 | loop fusion | flops 24576 | bytes 131328 | tf_op jit(solution)/shard_map/transpose | solution.py:89
  6.4 3.3 %reshape.514 = bf16[8,256,4,64]{3,2,1,0:T(4,128)(2,1)S(1)} reshape(bf16[2048,256]{1,0:T(8,128)(2,1)} %param.10) | data formatting | bytes 2097152 | tf_op jit(solution)/shard_map/reshape | solution.py:98
  9.7 1.0 copy.146
  10.9 1.0 copy.149
  12.0 2.4 %convolution_bitcast_fusion = f32[8,4,64,64]{2,3,1,0:T(8,128)} fusion(bf16[8,256,4,64]{1,3,2,0:T(8,128)(2,1)S(1)} %copy.146, f32[8,256,64]{1,2,0:T(8,128)} %copy.149, f32[4,8,256]{2,0,1:T(4,128)S(1)} %copy-done.20), kind=kOutput, calls=%fused_computation.28 | convolution fusion | flops 68157440 | bytes 2129920 | tf_op jit(solution)/shard_map/bshp,hbsn->bhpn/dot_general | solution.py:108
  14.4 9.3 %while.13 = (s32[]{:T(128)}, f32[4,64,64]{2,1,0:T(8,128)S(1)}, f32[8,4,64,64]{3,2,1,0:T(8,128)S(1)}, f32[8,4]{1,0:T(8,128)S(1)}, f32[8,4,64,64]{2,3,1,0:T(8,128)}, /*index=5*/s32[]{:T(128)}, s32[]{:T(128)}) while((s32[]{:T(128)}, f32[4,64,64]{2,1,0:T(8,128)S(1)}, f32[8,4,64,64]{3,2,1,0:T(8,128)S(1)}, f32[8,4]{1,0:T(8,128)S(1)}, ...), condition=%wide.region_3.4_spmd.clone, body=%wide.region_2.3_spmd.clone.sunk | while | flops 65539 | bytes 721044 | solution.py:116
  14.5 0.9 constant_dynamic-slice_fusion.3
  15.6 0.9 constant_dynamic-slice_fusion.3
  16.8 0.9 constant_dynamic-slice_fusion.3
  18.0 0.9 constant_dynamic-slice_fusion.3
  19.1 0.9 constant_dynamic-slice_fusion.3
  20.3 0.9 constant_dynamic-slice_fusion.3
  21.5 0.9 constant_dynamic-slice_fusion.3
  23.9 2.0 %all-gather.3 = f32[2,5,4096]{2,1,0:T(8,128)S(1)} all-gather(f32[1,5,4096]{2,1,0:T(8,128)S(1)} %maximum_bitcast_fusion), channel_id=2, replica_groups=mesh['seq_0'=8,'seq_1'=4,'seq_2'=2,'chan'=8] {'seq_2'}, dimensions={0}, use_global_device_ids=true | all-gather | bytes 245760 | tf_op jit(solution)/shard_map/all_gather | solution.py:29
  26.2 15.8 %all-gather.4 = f32[4,5,4096]{2,1,0:T(8,128)S(1)} all-gather(f32[1,5,4096]{2,1,0:T(8,128)S(1)} %maximum_bitcast_fusion.1), channel_id=3, replica_groups=mesh['seq_0'=8,'seq_1'=4,'seq_2'=2,'chan'=8] {'seq_1'}, dimensions={0}, use_global_device_ids=true | all-gather | bytes 409600 | tf_op jit(solution)/shard_map/all_gather | solution.py:29
  43.3 26.6 %all-gather.5 = f32[8,5,4096]{2,1,0:T(8,128)S(1)} all-gather(f32[1,5,4096]{2,1,0:T(8,128)S(1)} %maximum_bitcast_fusion.2), channel_id=4, replica_groups=mesh['seq_0'=8,'seq_1'=4,'seq_2'=2,'chan'=8] {'seq_0'}, dimensions={0}, use_global_device_ids=true | all-gather | bytes 737280 | tf_op jit(solution)/shard_map/all_gather | solution.py:29
  72.9 1.0 copy.188
  73.9 1.8 %fusion.18 = f32[8,4,64,256]{3,2,1,0:T(8,128)} fusion(f32[8,4,64,64]{3,2,1,0:T(8,128)S(1)} %get-tuple-element.33, bf16[8,256,64,1]{1,0,2,3:T(8,128)(2,1)S(1)} %bitcast.164), kind=kOutput, calls=%fused_computation.32 | convolution fusion | flops 67633152 | bytes 2883584 | tf_op jit(solution)/shard_map/btn,bhpn->bthp/dot_general | solution.py:86
  75.7 1.8 %fusion.29 = f32[8,4,64,256]{3,2,1,0:T(8,128)} fusion(f32[8,4,64,64]{3,2,1,0:T(8,128)S(1)} %get-tuple-element.33, bf16[8,256,64,1]{1,0,2,3:T(8,128)(2,1)S(1)} %bitcast.165), kind=kOutput, calls=%fused_computation.44 | convolution fusion | flops 67239936 | bytes 2883584 | tf_op jit(solution)/shard_map/btn,bhpn->bthp/dot_general | solution.py:83
  80.5 1.2 exp.208
  81.7 1.0 squeeze.92
  82.7 1.0 squeeze.93
  83.6 1.0 squeeze.94
  84.6 1.0 squeeze.95
  85.8 1.1 subtract_convert_fusion.2
  89.6 3.3 %fusion.14 = f32[8,256,4,64]{1,3,2,0:T(8,128)S(1)} fusion(bf16[8,256,4,64]{1,3,2,0:T(8,128)(2,1)S(1)} %copy.146, f32[8,4,64,256]{3,2,1,0:T(8,128)S(1)} %fusion.26, f32[8,4,64,256]{3,2,1,0:T(8,128)S(1)} %fusion.24, f32[8,4,64,256]{3,2,1,0:T(8,128)S(1)} %copy-done.2, f32[8,4,64,256]{3,2,1,0:T(8,128)S(1)} %copy-done.1, f32[4,8,256]{2,0,1:T(4,128)S(1)} %bitcast.181, ...), kind=kOutput, calls=%fused_computation.22 | convolution fusion | flops 285736960 | bytes 13828112 | tf_op jit(solution)/shard_map/hbts,bshp->bthp/dot_general | solution.py:131
  92.9 1.2 %copy.161 = f32[8,256,4,64]{1,0,3,2:T(8,128)S(1)} copy(f32[8,256,4,64]{1,3,2,0:T(8,128)S(1)} %fusion.14) | data formatting | bytes 4194304 | tf_op jit(solution)/shard_map/add | solution.py:137
  95.0 1.5 %copy.162 = bf16[2048,256]{0,1:T(8,128)(2,1)S(1)} copy(bf16[2048,256]{1,0:T(8,128)(2,1)} %param.11) | data formatting | bytes 2097152 | tf_op args[1]
  97.4 18.1 %all_to_all.6 = f32[8,1,2048]{2,1,0:T(1,128)S(1)} all-to-all(f32[8,1,2048]{2,1,0:T(1,128)S(1)} %broadcast_in_dim.42), channel_id=1, replica_groups=mesh['seq_0'=8,'seq_1'=4,'seq_2'=2,'chan'=8] {'chan'}, dimensions={0} | all-to-all | bytes 131072 | tf_op jit(solution)/shard_map/all_to_all | solution.py:55
  115.6 1.8 %multiply_convert_fusion.2 = bf16[2048,256]{0,1:T(8,128)(2,1)} fusion(f32[256]{0:T(256)S(1)} %copy-done.26, f32[2048]{0:T(1024)S(1)} %add_rsqrt_fusion, f32[2048,256]{0,1:T(8,128)S(1)} %bitcast.162, bf16[2048,256]{0,1:T(8,128)(2,1)S(1)} %copy.162), kind=kLoop, calls=%fused_computation.25 | loop fusion | flops 4718592 | bytes 4203520 | tf_op jit(solution)/shard_map/convert_element_type | solution.py:143
  117.4 2.3 %copy.164 = bf16[2048,256]{1,0:T(8,128)(2,1)} copy(bf16[2048,256]{0,1:T(8,128)(2,1)} %multiply_convert_fusion.2) | data formatting | bytes 2097152 | tf_op jit(solution)/shard_map/convert_element_type | solution.py:143
  (150 shorter events, 17.7 us)
Async XLA Ops:
  4.0 1.8 %copy-start.6 = (f32[4,8,256]{2,1,0:T(8,128)}, f32[4,8,256]{2,1,0:T(8,128)S(1)}, u32[]{:S(2)}) copy-start(f32[4,8,256]{2,1,0:T(8,128)S(1)} %get-tuple-element.97) | copy-start | bytes 98308
  9.7 1.1 copy-start.3
  10.8 1.2 %copy-start.20 = (f32[4,8,256]{2,0,1:T(4,128)S(1)}, f32[4,8,256]{2,0,1:T(4,128)}, u32[]{:S(2)}) copy-start(f32[4,8,256]{2,0,1:T(4,128)} %copy.148) | copy-start | bytes 98308
  10.9 3.6 %copy-start = (f32[8,4,64,64]{3,2,1,0:T(8,128)S(1)}, f32[8,4,64,64]{3,2,1,0:T(8,128)}, u32[]{:S(2)}) copy-start(f32[8,4,64,64]{3,2,1,0:T(8,128)} %custom-call.1) | copy-start | bytes 1572868
  42.7 0.5 copy-start.24
  42.7 0.6 copy-start.25
  75.6 1.8 %copy-start.7 = (f32[4,8,256]{2,1,0:T(8,128)S(1)}, f32[4,8,256]{2,1,0:T(8,128)}, u32[]{:S(2)}) copy-start(f32[4,8,256]{2,1,0:T(8,128)} %copy-done.6) | copy-start | bytes 98308
  75.6 3.1 %copy-start.15 = (f32[1,4,4096]{2,1,0:T(4,128)S(1)}, f32[1,4,4096]{2,1,0:T(4,128)}, u32[]{:S(2)}) copy-start(f32[1,4,4096]{2,1,0:T(4,128)} %get-tuple-element.103) | copy-start | bytes 196612
  75.7 3.2 %copy-start.14 = (f32[1,4,4096]{2,1,0:T(4,128)S(1)}, f32[1,4,4096]{2,1,0:T(4,128)}, u32[]{:S(2)}) copy-start(f32[1,4,4096]{2,1,0:T(4,128)} %get-tuple-element.109) | copy-start | bytes 196612
  75.7 3.4 %copy-start.13 = (f32[1,4,4096]{2,1,0:T(4,128)S(1)}, f32[1,4,4096]{2,1,0:T(4,128)}, u32[]{:S(2)}) copy-start(f32[1,4,4096]{2,1,0:T(4,128)} %get-tuple-element.108) | copy-start | bytes 196612
  75.7 3.5 %copy-start.12 = (f32[1,4,4096]{2,1,0:T(4,128)S(1)}, f32[1,4,4096]{2,1,0:T(4,128)}, u32[]{:S(2)}) copy-start(f32[1,4,4096]{2,1,0:T(4,128)} %get-tuple-element.107) | copy-start | bytes 196612
  75.7 3.6 %copy-start.11 = (f32[1,4,4096]{2,1,0:T(4,128)S(1)}, f32[1,4,4096]{2,1,0:T(4,128)}, u32[]{:S(2)}) copy-start(f32[1,4,4096]{2,1,0:T(4,128)} %get-tuple-element.106) | copy-start | bytes 196612
  75.7 3.7 %copy-start.10 = (f32[1,4,4096]{2,1,0:T(4,128)S(1)}, f32[1,4,4096]{2,1,0:T(4,128)}, u32[]{:S(2)}) copy-start(f32[1,4,4096]{2,1,0:T(4,128)} %get-tuple-element.105) | copy-start | bytes 196612
  75.7 3.8 %copy-start.9 = (f32[1,4,4096]{2,1,0:T(4,128)S(1)}, f32[1,4,4096]{2,1,0:T(4,128)}, u32[]{:S(2)}) copy-start(f32[1,4,4096]{2,1,0:T(4,128)} %get-tuple-element.104) | copy-start | bytes 196612
  75.7 4.0 %copy-start.8 = (f32[1,4,4096]{2,1,0:T(4,128)S(1)}, f32[1,4,4096]{2,1,0:T(4,128)}, u32[]{:S(2)}) copy-start(f32[1,4,4096]{2,1,0:T(4,128)} %get-tuple-element.110) | copy-start | bytes 196612
  75.7 4.1 %copy-start.5 = (f32[8,1,4096]{2,1,0:T(1,128)S(1)}, f32[8,1,4096]{2,1,0:T(1,128)}, u32[]{:S(2)}) copy-start(f32[8,1,4096]{2,1,0:T(1,128)} %slice.187) | copy-start | bytes 393220
  77.5 8.1 %copy-start.17 = (f32[1,4,4096]{2,1,0:T(4,128)S(1)}, f32[1,4,4096]{2,1,0:T(4,128)}, u32[]{:S(2)}) copy-start(f32[1,4,4096]{2,1,0:T(4,128)} %get-tuple-element.115) | copy-start | bytes 196612
  77.5 8.2 %copy-start.16 = (f32[1,4,4096]{2,1,0:T(4,128)S(1)}, f32[1,4,4096]{2,1,0:T(4,128)}, u32[]{:S(2)}) copy-start(f32[1,4,4096]{2,1,0:T(4,128)} %get-tuple-element.116) | copy-start | bytes 196612
  86.9 0.9 copy-start.19
  86.9 1.0 copy-start.18
  87.0 1.0 copy-start.4
  87.4 1.6 %copy-start.1 = (f32[8,4,64,256]{3,2,1,0:T(8,128)S(1)}, f32[8,4,64,256]{3,2,1,0:T(8,128)}, u32[]{:S(2)}) copy-start(f32[8,4,64,256]{3,2,1,0:T(8,128)} %fusion.18) | copy-start | bytes 6291460
  87.4 2.2 %copy-start.2 = (f32[8,4,64,256]{3,2,1,0:T(8,128)S(1)}, f32[8,4,64,256]{3,2,1,0:T(8,128)}, u32[]{:S(2)}) copy-start(f32[8,4,64,256]{3,2,1,0:T(8,128)} %fusion.29) | copy-start | bytes 6291460
  87.4 2.2 %copy-start.21 = (pred[256,256]{1,0:T(8,128)(4,1)S(1)}, pred[256,256]{1,0:T(8,128)(4,1)}, u32[]{:S(2)}) copy-start(pred[256,256]{1,0:T(8,128)(4,1)} %iota_compare_fusion) | copy-start | bytes 196612
  87.4 2.2 %copy-start.22 = (f32[4,8,256]{2,0,1:T(4,128)S(1)}, f32[4,8,256]{2,0,1:T(4,128)}, u32[]{:S(2)}) copy-start(f32[4,8,256]{2,0,1:T(4,128)} %copy.142) | copy-start | bytes 98308
  87.4 2.2 %copy-start.23 = (f32[4,2048]{1,0:T(4,128)S(1)}, f32[4,2048]{1,0:T(4,128)}, u32[]{:S(2)}) copy-start(f32[4,2048]{1,0:T(4,128)} %param.14) | copy-start | bytes 98308
  87.4 2.2 %copy-start.27 = (f32[4]{0:T(128)S(1)}, f32[4]{0:T(128)}, u32[]{:S(2)}) copy-start(f32[4]{0:T(128)} %param.16) | copy-start | bytes 52
  96.5 19.1 %copy-start.26 = (f32[256]{0:T(256)S(1)}, f32[256]{0:T(256)}, u32[]{:S(2)}) copy-start(f32[256]{0:T(256)} %param.17) | copy-start | bytes 3076
where the time goes:
time: 120 us
  blocking collectives  62.5 us (52%)
  local copies, waits for them, and re-layouts  34.4 us (29%)
  other arithmetic  11.4 us (10%)
  matrix products  10.5 us (9%)
    all_gather x3, blocking collectives, all_in_one(): both, at, found = (lax.all_gather(jnp.concatenate(lines), axis), 0, {})  44.3 us
    all_to_all x1, blocking collectives, copy_for_each(): lax.all_to_all(jnp.broadcast_to(shard[None], (length, *shard.shape)), axi...  18.1 us
    dynamic_slice x16, local copies, waits for them, and re-layouts, per_device(): lax.scan(carry_blocks, jnp.zeros((head_count, head_width, nstate), jnp.fl...  8.12 us
    unnamed x64, local copies, waits for them, and re-layouts  5.44 us
    squeeze x14, local copies, waits for them, and re-layouts, prefix_by_axis(): total = combine(total, jax.tree.map(lambda part: part[k], pieces))  5.12 us
    reshape x2, local copies, waits for them, and re-layouts, per_device(): x_blocks = x_in.reshape(block_count, BLOCK, head_count, head_width)  4.35 us
    dot_general x1, matrix products, per_device(): jnp.einsum('hbts,bshp->bthp', weights, x_blocks, preferred_element_type=j...  3.28 us
    dot_general x1, matrix products, per_device(): jnp.einsum('bshp,hbsn->bhpn', x_blocks, decayed_b, preferred_element_type...  2.44 us

commit v1 on v0

v1 whole, which is shorter than its diff:
```python
import functools

import jax
import jax.numpy as jnp
from jax import lax
from jax.experimental import pallas as pl
from jax.experimental.pallas import tpu as pltpu
from jax.sharding import PartitionSpec as P

BLOCK = 256
LANES = 128
EPSILON = 1e-05
GROUP = 8
MESH = pl.DeviceIdType.MESH
F32 = jnp.float32
BF16 = jnp.bfloat16


def split2(v):
    high = v.astype(BF16)
    return high, (v - high.astype(F32)).astype(BF16)


def dot(a, b, contract=((1,), (0,))):
    return lax.dot_general(a, b, (contract, ((), ())), preferred_element_type=F32)


def layer(
    group, rows_y, nchan,
    x_hbm, gate_hbm, b_hbm, c_hbm, step_hbm, keep_hbm, skip_hbm, gain_hbm,
    out_hbm,
    x_s, gate_s, b_s, c_s, step_s, keep_s, skip_s, gain_s,
    keep8, step8, cum8, c2_s,
    totals, device_total, block_state, starts, prefix_s,
    end_s, gather1, totals1, group_prefix, group_total_state, group_total,
    gather2, totals2, entering_s, back_s, gather3,
    base_s, slope_s, squares_s, gather_sq, out_s,
    load_sem, skip_sem, store_sem,
    sa_send, sa_recv, sb_send, sb_recv, sc_send, sc_recv,
    sd_send, sd_recv, se_send, se_recv, sf_send, sf_recv,
):
    tokens, channels = x_s.shape
    nstate = b_s.shape[0]
    heads = keep_s.shape[0]
    width = channels // heads
    blocks = tokens // BLOCK
    tiles = channels // LANES
    per_tile = heads // tiles
    piece = nstate // group

    me = lax.axis_index("seq")
    me_z = lax.axis_index("chan")
    me_y = me // group
    me_j = me % group

    loads = [
        pltpu.make_async_copy(src, dst, load_sem.at[i])
        for i, (src, dst) in enumerate(
            (
                (keep_hbm, keep_s), (step_hbm, step_s), (b_hbm, b_s), (x_hbm, x_s),
                (c_hbm, c_s), (gate_hbm, gate_s), (gain_hbm, gain_s),
            )
        )
    ]
    loads.append(pltpu.make_async_copy(skip_hbm, skip_s, skip_sem))
    for copy in loads:
        copy.start()

    def in_group(i):
        return (me_j + i) % group

    def at_group(j):
        return (me_y * group + j, me_z)

    def at_y(y):
        return (y * group + me_j, me_z)

    barrier = pltpu.get_barrier_semaphore()
    for i in range(1, group):
        pl.semaphore_signal(barrier, inc=1, device_id=at_group(in_group(i)), device_id_type=MESH)
    for i in range(1, rows_y):
        pl.semaphore_signal(
            barrier, inc=1, device_id=at_y((me_y + i) % rows_y), device_id_type=MESH
        )
    for i in range(1, nchan):
        pl.semaphore_signal(
            barrier, inc=1, device_id=(me, (me_z + i) % nchan), device_id_type=MESH
        )

    lane = lax.broadcasted_iota(jnp.int32, (8, channels), 1)
    row8 = lax.broadcasted_iota(jnp.int32, (8, channels), 0)
    own_head = (lane // width) == row8
    half = lax.broadcasted_iota(jnp.int32, (1, LANES), 1) < width
    upper = (
        lax.broadcasted_iota(jnp.int32, (BLOCK, BLOCK), 0)
        <= lax.broadcasted_iota(jnp.int32, (BLOCK, BLOCK), 1)
    )
    upper = jnp.where(upper, 1.0, 0.0).astype(BF16)

    loads[0].wait()
    loads[1].wait()
    keep8[...] = jnp.zeros_like(keep8)
    step8[...] = jnp.zeros_like(step8)
    for k in range(blocks):
        keep8[8 * k : 8 * k + heads, :] = keep_s[:, BLOCK * k : BLOCK * (k + 1)]
        step8[8 * k : 8 * k + heads, :] = step_s[:, BLOCK * k : BLOCK * (k + 1)]
    keep = keep8[...]
    k_high = keep.astype(BF16)
    rest = keep - k_high.astype(F32)
    k_mid, k_low = split2(rest)
    cum8[...] = dot(k_high, upper) + (dot(k_mid, upper) + dot(k_low, upper))

    for k in range(blocks):
        last = cum8[8 * k : 8 * k + 8, BLOCK - 1 : BLOCK]
        spread = jnp.where(own_head, jnp.broadcast_to(last, (8, channels)), 0.0)
        totals[k : k + 1, :] = jnp.sum(spread, axis=0, keepdims=True)
    device_total[...] = jnp.broadcast_to(
        jnp.sum(totals[...], axis=0, keepdims=True), device_total.shape
    )

    pl.semaphore_wait(barrier, group + rows_y + nchan - 3)

    def copy_a(i):
        return pltpu.make_async_remote_copy(
            device_total, totals1.at[me_j], sa_send.at[i], sa_recv.at[me_j],
            device_id=at_group(in_group(i)), device_id_type=MESH,
        )

    for i in range(1, group):
        copy_a(i).start()

    loads[2].wait()
    loads[3].wait()
    for k in range(blocks):
        slab = cum8[8 * k : 8 * k + 8, :]
        coef = jnp.exp(slab[:, BLOCK - 1 : BLOCK] - slab) * step8[8 * k : 8 * k + 8, :]
        bt = b_s[:, BLOCK * k : BLOCK * (k + 1)].astype(F32)
        for t in range(tiles):
            left = jnp.concatenate(
                [(bt * coef[h : h + 1, :]).astype(BF16) for h in (2 * t, 2 * t + 1)], axis=0
            )
            both = dot(left, x_s[BLOCK * k : BLOCK * (k + 1), LANES * t : LANES * (t + 1)])
            block_state[k, :, LANES * t : LANES * (t + 1)] = jnp.where(
                half, both[:nstate], both[nstate:]
            )
    running = jnp.zeros((nstate, channels), F32)
    for k in range(blocks):
        starts[k] = running
        running = jnp.exp(totals[k : k + 1, :]) * running + block_state[k]
    for p in range(group):
        end_s[p] = running[piece * p : piece * (p + 1), :]

    def copy_b(i):
        p = in_group(i)
        return pltpu.make_async_remote_copy(
            end_s.at[p], gather1.at[me_j], sb_send.at[i], sb_recv.at[me_j],
            device_id=at_group(p), device_id_type=MESH,
        )

    for i in range(1, group):
        copy_b(i).start()
    gather1[me_j] = end_s[me_j]
    totals1[me_j] = device_total[...]

    before = jnp.zeros((1, channels), F32)
    for k in range(blocks):
        prefix_s[k : k + 1, :] = before
        before = before + totals[k : k + 1, :]

    for i in range(4, len(loads)):
        loads[i].wait()
    head_of = lax.broadcasted_iota(jnp.int32, (1, channels), 1) // width
    skip_row = jnp.zeros((1, channels), F32)
    for h in range(heads):
        skip_row = jnp.where(head_of == h, skip_s[0, h], skip_row)
    diagonal = (
        lax.broadcasted_iota(jnp.int32, (LANES, LANES), 0)
        >= lax.broadcasted_iota(jnp.int32, (LANES, LANES), 1)
    )

    def inside(k, carry):
        rows = pl.ds(pl.multiple_of(k * BLOCK, BLOCK), BLOCK)
        slab_at = pl.ds(pl.multiple_of(k * 8, 8), 8)
        slab = cum8[slab_at, :]
        steps = step8[slab_at, :]
        columns = jnp.transpose(slab)
        c_block = c_s[:, rows]
        c_pair = jnp.transpose(jnp.concatenate([c_block, c_block], axis=0))
        c2_s[rows, :] = c_pair
        scores = dot(c_pair[:, :nstate], b_s[:, rows])
        for t in range(tiles):
            lanes = slice(LANES * t, LANES * (t + 1))
            weights, spreads = [], []
            for h in (2 * t, 2 * t + 1):
                column = jnp.broadcast_to(columns[:, h : h + 1], (BLOCK, LANES))
                spreads.append(column)

                def weight(r, s):
                    rr, ss = slice(LANES * r, LANES * (r + 1)), slice(LANES * s, LANES * (s + 1))
                    w = (
                        scores[rr, ss]
                        * jnp.exp(column[rr, :] - slab[h : h + 1, ss])
                        * steps[h : h + 1, ss]
                    )
                    return (jnp.where(diagonal, w, 0.0) if r == s else w).astype(BF16)

                top = jnp.concatenate([weight(0, 0), jnp.zeros((LANES, LANES), BF16)], axis=1)
                bottom = jnp.concatenate([weight(1, 0), weight(1, 1)], axis=1)
                weights += [top, bottom]
            x_tile = x_s[rows, lanes]
            both = dot(jnp.concatenate(weights, axis=0), x_tile)
            value = jnp.where(half, both[:BLOCK], both[BLOCK:])
            value = value + skip_row[:, lanes] * x_tile.astype(F32)
            gate = gate_s[rows, lanes].astype(F32)
            gate = gate / (1.0 + jnp.exp(-gate))
            base_s[rows, lanes] = value * gate
            slope_s[rows, lanes] = jnp.exp(jnp.where(half, spreads[0], spreads[1])) * gate
        return carry

    cuts = (0, (blocks * 3) // 8, (blocks * 6) // 8, blocks)
    lax.fori_loop(cuts[0], cuts[1], inside, 0)

    for m in range(group):

        @pl.when(m != me_j)
        def _():
            pltpu.make_async_remote_copy(
                device_total, totals1.at[m], sa_send.at[0], sa_recv.at[m],
                device_id=at_group(m), device_id_type=MESH,
            ).wait_recv()

    total = totals1[0]
    for m in range(1, group):
        total = total + totals1[m]
    group_total[...] = total

    def copy_c(i):
        return pltpu.make_async_remote_copy(
            group_total, totals2.at[me_y], sc_send.at[i], sc_recv.at[me_y],
            device_id=at_y(me_y + i), device_id_type=MESH,
        )

    def copy_d(i):
        return pltpu.make_async_remote_copy(
            group_total_state, gather2.at[me_y], sd_send.at[i], sd_recv.at[me_y],
            device_id=at_y(me_y + i), device_id_type=MESH,
        )

    for i in range(1, rows_y):

        @pl.when(me_y + i < rows_y)
        def _():
            copy_c(i).start()

    for m in range(group):

        @pl.when(m != me_j)
        def _():
            pltpu.make_async_remote_copy(
                end_s.at[m], gather1.at[m], sb_send.at[0], sb_recv.at[m],
                device_id=at_group(m), device_id_type=MESH,
            ).wait_recv()

    state = jnp.zeros((piece, channels), F32)
    for m in range(group):
        group_prefix[m] = state
        state = jnp.exp(totals1[m, 0:1, :]) * state + gather1[m]
    group_total_state[...] = state
    for i in range(1, rows_y):

        @pl.when(me_y + i < rows_y)
        def _():
            copy_d(i).start()

    lax.fori_loop(cuts[1], cuts[2], inside, 0)

    entering_s[...] = jnp.zeros_like(entering_s)
    for y in range(rows_y - 1):

        @pl.when(y < me_y)
        def _():
            pltpu.make_async_remote_copy(
                group_total, totals2.at[y], sc_send.at[0], sc_recv.at[y],
                device_id=at_y(y), device_id_type=MESH,
            ).wait_recv()
            pltpu.make_async_remote_copy(
                group_total_state, gather2.at[y], sd_send.at[0], sd_recv.at[y],
                device_id=at_y(y), device_id_type=MESH,
            ).wait_recv()
            entering_s[...] = jnp.exp(totals2[y, 0:1, :]) * entering_s[...] + gather2[y]

    entering = entering_s[...]
    ahead = jnp.zeros((1, channels), F32)
    for m in range(group):
        back_s[m] = jnp.exp(ahead) * entering + group_prefix[m]
        ahead = ahead + totals1[m, 0:1, :]

    def copy_e(i):
        p = in_group(i)
        return pltpu.make_async_remote_copy(
            back_s.at[p], gather3.at[me_j], se_send.at[i], se_recv.at[me_j],
            device_id=at_group(p), device_id_type=MESH,
        )

    for i in range(1, group):
        copy_e(i).start()
    gather3[me_j] = back_s[me_j]

    lax.fori_loop(cuts[2], cuts[3], inside, 0)

    for m in range(group):

        @pl.when(m != me_j)
        def _():
            pltpu.make_async_remote_copy(
                back_s.at[m], gather3.at[m], se_send.at[0], se_recv.at[m],
                device_id=at_group(m), device_id_type=MESH,
            ).wait_recv()

    incoming = jnp.concatenate([gather3[p] for p in range(group)], axis=0)
    ones = jnp.ones((8, BLOCK), BF16)
    for k in range(blocks):
        rows = slice(BLOCK * k, BLOCK * (k + 1))
        at_start = starts[k] + jnp.exp(prefix_s[k : k + 1, :]) * incoming
        high, low = split2(at_start)
        read = dot(c2_s[rows, :], jnp.concatenate([high, low], axis=0))
        gated = base_s[rows, :] + slope_s[rows, :] * read
        base_s[rows, :] = gated
        square = gated * gated
        partial = square[:, :LANES]
        for t in range(1, tiles):
            partial = partial + square[:, LANES * t : LANES * (t + 1)]
        high, low = split2(partial)
        row = dot(ones, jnp.concatenate([high, low], axis=1), ((1,), (1,)))
        squares_s[k : k + 1, :] = row[0:1, :]

    def copy_f(i):
        return pltpu.make_async_remote_copy(
            squares_s, gather_sq.at[me_z], sf_send.at[i], sf_recv.at[me_z],
            device_id=(me, (me_z + i) % nchan), device_id_type=MESH,
        )

    for i in range(1, nchan):
        copy_f(i).start()
    gather_sq[me_z] = squares_s[...]
    for z in range(nchan):

        @pl.when(z != me_z)
        def _():
            pltpu.make_async_remote_copy(
                squares_s, gather_sq.at[z], sf_send.at[0], sf_recv.at[z],
                device_id=(me, z), device_id_type=MESH,
            ).wait_recv()

    total = gather_sq[0]
    for z in range(1, nchan):
        total = total + gather_sq[z]
    factor = jnp.transpose(lax.rsqrt(total / (channels * nchan) + EPSILON))
    gain = gain_s[...]
    stores = []
    for k in range(blocks):
        rows = slice(BLOCK * k, BLOCK * (k + 1))
        scale = jnp.broadcast_to(factor[:, k : k + 1], (BLOCK, LANES))
        for t in range(tiles):
            lanes = slice(LANES * t, LANES * (t + 1))
            out_s[rows, lanes] = (base_s[rows, lanes] * scale * gain[:, lanes]).astype(BF16)
        store = pltpu.make_async_copy(out_s.at[rows, :], out_hbm.at[rows, :], store_sem.at[k])
        store.start()
        stores.append(store)

    for i in range(1, group):
        copy_a(i).wait_send()
        copy_b(i).wait_send()
        copy_e(i).wait_send()
    for i in range(1, rows_y):

        @pl.when(me_y + i < rows_y)
        def _():
            copy_c(i).wait_send()
            copy_d(i).wait_send()

    for i in range(1, nchan):
        copy_f(i).wait_send()
    for store in stores:
        store.wait()


def per_device(group, rows_y, nchan, x, gate, b, c, step, keep, skip, gain):
    tokens, channels = x.shape
    nstate = b.shape[1]
    heads = step.shape[0]
    blocks = tokens // BLOCK
    piece = nstate // group
    vmem = pltpu.VMEM
    dma = pltpu.SemaphoreType.DMA
    anywhere = pl.BlockSpec(memory_space=pl.ANY)
    scratch = [
        vmem((tokens, channels), BF16), vmem((tokens, channels), BF16),
        vmem((nstate, tokens), BF16), vmem((nstate, tokens), BF16),
        vmem((heads, tokens), F32), vmem((heads, tokens), F32),
        pltpu.SMEM((1, heads), F32), vmem((1, channels), F32),
        vmem((8 * blocks, BLOCK), F32), vmem((8 * blocks, BLOCK), F32),
        vmem((8 * blocks, BLOCK), F32),
        vmem((tokens, 2 * nstate), BF16),
        vmem((blocks, channels), F32), vmem((8, channels), F32),
        vmem((blocks, nstate, channels), F32), vmem((blocks, nstate, channels), F32),
        vmem((blocks, channels), F32),
        vmem((group, piece, channels), F32), vmem((group, piece, channels), F32),
        vmem((group, 8, channels), F32), vmem((group, piece, channels), F32),
        vmem((piece, channels), F32), vmem((8, channels), F32),
        vmem((rows_y, piece, channels), F32), vmem((rows_y, 8, channels), F32),
        vmem((piece, channels), F32),
        vmem((group, piece, channels), F32), vmem((group, piece, channels), F32),
        vmem((tokens, channels), F32), vmem((tokens, channels), F32),
        vmem((blocks, BLOCK), F32), vmem((nchan, blocks, BLOCK), F32),
        vmem((tokens, channels), BF16),
        dma((7,)), dma, dma((blocks,)),
        dma((group,)), dma((group,)), dma((group,)), dma((group,)),
        dma((rows_y,)), dma((rows_y,)), dma((rows_y,)), dma((rows_y,)),
        dma((group,)), dma((group,)), dma((nchan,)), dma((nchan,)),
    ]
    return pl.pallas_call(
        functools.partial(layer, group, rows_y, nchan),
        out_shape=jax.ShapeDtypeStruct((tokens, channels), BF16),
        in_specs=[anywhere] * 8,
        out_specs=anywhere,
        scratch_shapes=scratch,
        compiler_params=pltpu.CompilerParams(collective_id=0, has_side_effects=True),
    )(x, gate, b.T, c.T, step, keep, skip.reshape(1, heads), gain.reshape(1, channels))


def build(mesh, group):
    rows_y = mesh.shape["seq"] // group
    placed = (
        P("seq", "chan"), P("seq", "chan"), P("seq", None), P("seq", None),
        P("chan", "seq"), P("chan", "seq"), P("chan"), P("chan"),
    )
    return jax.shard_map(
        functools.partial(per_device, group, rows_y, mesh.shape["chan"]),
        mesh=mesh, in_specs=placed, out_specs=P("seq", "chan"), check_vma=False,
    )


def solution(mesh):
    return build(mesh, GROUP)
```

time: 120 us -> 35 us (0.29)
  the two profiles are of different devices: /device:TPU:2 before, /device:TPU:56 now
where the time goes in v1:
time: 35 us; the launch traced here: 34.8 us
  Pallas kernels  32.5 us (93%)
  local copies, waits for them, and re-layouts  2.26 us (6%)
    pallas_call x1, Pallas kernels, per_device(): pl.pallas_call(functools.partial(layer, group, rows_y, nchan), out_shape=...  32.5 us
    unnamed x1, local copies, waits for them, and re-layouts  2.26 us

profile of v1, /device:TPU:56, one launch (start us, length us, event | category | flops | bytes accessed | tf_op | source)
XLA Modules:
  0.0 34.8 jit_solution(2354402261111792027)
XLA Ops:
  0.0 32.5 %shard_map.82 = bf16[2048,256]{1,0:T(8,128)(2,1)} custom-call(bf16[2048,256]{1,0:T(8,128)(2,1)} %x_hbm.1, bf16[2048,256]{1,0:T(8,128)(2,1)} %gate_hbm.1, bf16[64,2048]{1,0:T(8,128)(2,1)} %bitcast.4, bf16[64,2048]{1,0:T(8,128)(2,1)} %bitcast.5, f32[4,2048]{1,0:T(4,128)} %step_hbm.1, f32[4,2048]{1,0:T(4,128)} %keep_hbm.1, f32[1,4]{1,0:T(1,128)} %bitcast.7, ...), custom_call_target="tpu_custom_call" | custom-call | tf_op jit(solution)/shard_map/pallas_call | solution.py:422
  32.5 2.3 %copy.10 = bf16[2048,256]{1,0:T(8,128)(2,1)} copy(bf16[2048,256]{1,0:T(8,128)(2,1)} %shard_map.82) | data formatting | bytes 2097152

commit v2 on v1

v2 whole, which is shorter than its diff:
```python
import functools

import jax
import jax.numpy as jnp
from jax import lax
from jax.experimental import pallas as pl
from jax.experimental.pallas import tpu as pltpu
from jax.sharding import PartitionSpec as P

BLOCK = 256
LANES = 128
EPSILON = 1e-05
GROUP = 8
MESH = pl.DeviceIdType.MESH
F32 = jnp.float32
BF16 = jnp.bfloat16


def split2(v):
    high = v.astype(BF16)
    return high, (v - high.astype(F32)).astype(BF16)


def dot(a, b, contract=((1,), (0,))):
    return lax.dot_general(a, b, (contract, ((), ())), preferred_element_type=F32)


def layer(
    group, rows_y, nchan,
    x_hbm, gate_hbm, b_hbm, c_hbm, step_hbm, keep_hbm, skip_hbm, gain_hbm,
    out_ref,
    x_s, gate_s, b_s, c_s, step_s, keep_s, skip_s, gain_s,
    keep8, step8, cum8, c2_s,
    totals, device_total, block_state, starts, prefix_s,
    end_s, gather1, totals1, group_prefix, group_total_state, group_total,
    gather2, totals2, entering_s, back_s, gather3,
    base_s, slope_s, squares_s, gather_sq,
    load_sem, skip_sem, y_in, z_in,
    sa_send, sa_recv, sb_send, sb_recv, sc_send, sc_recv,
    sd_send, sd_recv, se_send, se_recv, sf_send, sf_recv,
):
    tokens, channels = x_s.shape
    nstate = b_s.shape[0]
    heads = keep_s.shape[0]
    width = channels // heads
    blocks = tokens // BLOCK
    tiles = channels // LANES
    per_tile = heads // tiles
    piece = 2 * nstate // group

    me = lax.axis_index("seq")
    me_z = lax.axis_index("chan")
    me_y = me // group
    me_j = me % group
    is_owner = me_j % 2 == 1
    me_q = me_j // 2

    def owner(q):
        return 2 * q + 1

    def at_group(j):
        return (me_y * group + j, me_z)

    def at_y(y):
        return (y * group + me_j, me_z)

    def rank(y):
        return jnp.minimum(y, rows_y - y) * rows_y + y

    barrier = pltpu.get_barrier_semaphore()

    def greet(device):
        pl.semaphore_signal(barrier, inc=1, device_id=device, device_id_type=MESH)

    def report(semaphore, device):
        pl.semaphore_signal(semaphore, inc=1, device_id=device, device_id_type=MESH)

    for j in range(group):

        @pl.when((j != me_j) & (is_owner | (j % 2 == 1)))
        def _():
            greet(at_group(j))

    for y in range(rows_y):

        @pl.when(is_owner & (rank(me_y) < rank(y)))
        def _():
            greet(at_y(y))

    for z in range(nchan):

        @pl.when(me_z < z)
        def _():
            greet((me, z))

    loads = [
        pltpu.make_async_copy(src, dst, load_sem.at[i])
        for i, (src, dst) in enumerate(
            (
                (keep_hbm, keep_s), (step_hbm, step_s), (b_hbm, b_s), (x_hbm, x_s),
                (c_hbm, c_s), (gate_hbm, gate_s), (gain_hbm, gain_s),
            )
        )
    ]
    loads.append(pltpu.make_async_copy(skip_hbm, skip_s, skip_sem))
    for copy in loads:
        copy.start()

    lane = lax.broadcasted_iota(jnp.int32, (8, channels), 1)
    row8 = lax.broadcasted_iota(jnp.int32, (8, channels), 0)
    own_head = (lane // width) == row8
    half = lax.broadcasted_iota(jnp.int32, (1, LANES), 1) < width
    upper = (
        lax.broadcasted_iota(jnp.int32, (BLOCK, BLOCK), 0)
        <= lax.broadcasted_iota(jnp.int32, (BLOCK, BLOCK), 1)
    )
    upper = jnp.where(upper, 1.0, 0.0).astype(BF16)

    loads[0].wait()
    loads[1].wait()
    keep8[...] = jnp.zeros_like(keep8)
    step8[...] = jnp.zeros_like(step8)
    for k in range(blocks):
        keep8[8 * k : 8 * k + heads, :] = keep_s[:, BLOCK * k : BLOCK * (k + 1)]
        step8[8 * k : 8 * k + heads, :] = step_s[:, BLOCK * k : BLOCK * (k + 1)]
    keep = keep8[...]
    k_high = keep.astype(BF16)
    rest = keep - k_high.astype(F32)
    k_mid, k_low = split2(rest)
    cum8[...] = dot(k_high, upper) + (dot(k_mid, upper) + dot(k_low, upper))

    for k in range(blocks):
        last = cum8[8 * k : 8 * k + 8, BLOCK - 1 : BLOCK]
        spread = jnp.where(own_head, jnp.broadcast_to(last, (8, channels)), 0.0)
        totals[k : k + 1, :] = jnp.sum(spread, axis=0, keepdims=True)
    device_total[...] = jnp.sum(totals[...], axis=0, keepdims=True)

    loads[2].wait()
    loads[3].wait()
    for k in range(blocks):
        slab = cum8[8 * k : 8 * k + 8, :]
        coef = jnp.exp(slab[:, BLOCK - 1 : BLOCK] - slab) * step8[8 * k : 8 * k + 8, :]
        bt = b_s[:, BLOCK * k : BLOCK * (k + 1)].astype(F32)
        for t in range(tiles):
            left = jnp.concatenate(
                [(bt * coef[h : h + 1, :]).astype(BF16) for h in (2 * t, 2 * t + 1)], axis=0
            )
            both = dot(left, x_s[BLOCK * k : BLOCK * (k + 1), LANES * t : LANES * (t + 1)])
            block_state[k, :, LANES * t : LANES * (t + 1)] = jnp.where(
                half, both[:nstate], both[nstate:]
            )
    running = jnp.zeros((nstate, channels), F32)
    for k in range(blocks):
        starts[k] = running
        running = jnp.exp(totals[k : k + 1, :]) * running + block_state[k]
    for q in range(group // 2):
        end_s[q] = running[piece * q : piece * (q + 1), :]

    greeted = me_z + jnp.where(is_owner, group - 1, group // 2)
    expected_y = 0
    for y in range(rows_y):
        greeted = greeted + jnp.where(is_owner & (rank(y) < rank(me_y)), 1, 0)
        expected_y = expected_y + jnp.where((y > me_y) & (rank(y) > rank(me_y)), 1, 0)
    pl.semaphore_wait(barrier, greeted)

    def copy_a(i):
        return pltpu.make_async_remote_copy(
            device_total, totals1.at[me_j], sa_send.at[i], sa_recv.at[me_j],
            device_id=at_group(owner((me_q + i) % (group // 2))), device_id_type=MESH,
        )

    def copy_b(i):
        q = (me_q + i) % (group // 2)
        return pltpu.make_async_remote_copy(
            end_s.at[q], gather1.at[me_j], sb_send.at[i], sb_recv.at[me_j],
            device_id=at_group(owner(q)), device_id_type=MESH,
        )

    others = [group // 4] + [i for i in range(group // 2) if i != group // 4]
    for i in others:

        @pl.when((i != 0) | jnp.logical_not(is_owner))
        def _():
            copy_a(i).start()
            copy_b(i).start()

    for z in range(nchan):

        @pl.when(z < me_z)
        def _():
            report(z_in, (me, z))

    for y in range(rows_y):

        @pl.when(is_owner & (y < me_y) & (rank(y) < rank(me_y)))
        def _():
            report(y_in, at_y(y))

    @pl.when(is_owner)
    def _():
        gather1[me_j] = end_s[me_q]
        totals1[me_j] = device_total[...]

    before = jnp.zeros((1, channels), F32)
    for k in range(blocks):
        prefix_s[k : k + 1, :] = before
        before = before + totals[k : k + 1, :]

    for i in range(4, len(loads)):
        loads[i].wait()
    head_of = lax.broadcasted_iota(jnp.int32, (1, channels), 1) // width
    skip_row = jnp.zeros((1, channels), F32)
    for h in range(heads):
        skip_row = jnp.where(head_of == h, skip_s[0, h], skip_row)
    diagonal = (
        lax.broadcasted_iota(jnp.int32, (LANES, LANES), 0)
        >= lax.broadcasted_iota(jnp.int32, (LANES, LANES), 1)
    )

    def inside(k, carry):
        rows = pl.ds(pl.multiple_of(k * BLOCK, BLOCK), BLOCK)
        slab_at = pl.ds(pl.multiple_of(k * 8, 8), 8)
        slab = cum8[slab_at, :]
        steps = step8[slab_at, :]
        columns = jnp.transpose(slab)
        c_block = c_s[:, rows]
        c_pair = jnp.transpose(jnp.concatenate([c_block, c_block], axis=0))
        c2_s[rows, :] = c_pair
        scores = dot(c_pair[:, :nstate], b_s[:, rows])
        for t in range(tiles):
            lanes = slice(LANES * t, LANES * (t + 1))
            weights, spreads = [], []
            for h in (2 * t, 2 * t + 1):
                column = jnp.broadcast_to(columns[:, h : h + 1], (BLOCK, LANES))
                spreads.append(column)

                def weight(r, s):
                    rr, ss = slice(LANES * r, LANES * (r + 1)), slice(LANES * s, LANES * (s + 1))
                    w = (
                        scores[rr, ss]
                        * jnp.exp(column[rr, :] - slab[h : h + 1, ss])
                        * steps[h : h + 1, ss]
                    )
                    return (jnp.where(diagonal, w, 0.0) if r == s else w).astype(BF16)

                top = jnp.concatenate([weight(0, 0), jnp.zeros((LANES, LANES), BF16)], axis=1)
                bottom = jnp.concatenate([weight(1, 0), weight(1, 1)], axis=1)
                weights += [top, bottom]
            x_tile = x_s[rows, lanes]
            both = dot(jnp.concatenate(weights, axis=0), x_tile)
            value = jnp.where(half, both[:BLOCK], both[BLOCK:])
            value = value + skip_row[:, lanes] * x_tile.astype(F32)
            gate = gate_s[rows, lanes].astype(F32)
            gate = gate / (1.0 + jnp.exp(-gate))
            base_s[rows, lanes] = value * gate
            slope_s[rows, lanes] = jnp.exp(jnp.where(half, spreads[0], spreads[1])) * gate
        return carry

    cuts = (0, blocks // 2, blocks)
    lax.fori_loop(cuts[0], cuts[1], inside, 0)

    def copy_c(i):
        return pltpu.make_async_remote_copy(
            group_total, totals2.at[me_y], sc_send.at[i], sc_recv.at[me_y],
            device_id=at_y(me_y + i), device_id_type=MESH,
        )

    def copy_d(i):
        return pltpu.make_async_remote_copy(
            group_total_state, gather2.at[me_y], sd_send.at[i], sd_recv.at[me_y],
            device_id=at_y(me_y + i), device_id_type=MESH,
        )

    @pl.when(is_owner)
    def _():
        @pl.when(expected_y > 0)
        def _():
            pl.semaphore_wait(y_in, expected_y)

        for m in range(group):

            @pl.when(m != me_j)
            def _():
                pltpu.make_async_remote_copy(
                    device_total, totals1.at[m], sa_send.at[0], sa_recv.at[m],
                    device_id=at_group(m), device_id_type=MESH,
                ).wait_recv()

        total = totals1[0]
        for m in range(1, group):
            total = total + totals1[m]
        group_total[...] = total
        for i in range(1, rows_y):

            @pl.when(me_y + i < rows_y)
            def _():
                copy_c(i).start()

        for m in range(group):

            @pl.when(m != me_j)
            def _():
                pltpu.make_async_remote_copy(
                    end_s.at[0], gather1.at[m], sb_send.at[0], sb_recv.at[m],
                    device_id=at_group(m), device_id_type=MESH,
                ).wait_recv()

        state = jnp.zeros((piece, channels), F32)
        for m in range(group):
            group_prefix[m] = state
            state = jnp.exp(totals1[m]) * state + gather1[m]
        group_total_state[...] = state
        for i in range(1, rows_y):

            @pl.when(me_y + i < rows_y)
            def _():
                copy_d(i).start()


    def copy_e(i):
        p = (me_j + i) % group
        return pltpu.make_async_remote_copy(
            back_s.at[p], gather3.at[me_q], se_send.at[i], se_recv.at[me_q],
            device_id=at_group(p), device_id_type=MESH,
        )

    @pl.when(is_owner)
    def _():
        entering_s[...] = jnp.zeros_like(entering_s)
        for y in range(rows_y - 1):

            @pl.when(y < me_y)
            def _():
                pltpu.make_async_remote_copy(
                    group_total, totals2.at[y], sc_send.at[0], sc_recv.at[y],
                    device_id=at_y(y), device_id_type=MESH,
                ).wait_recv()
                pltpu.make_async_remote_copy(
                    group_total_state, gather2.at[y], sd_send.at[0], sd_recv.at[y],
                    device_id=at_y(y), device_id_type=MESH,
                ).wait_recv()
                entering_s[...] = jnp.exp(totals2[y]) * entering_s[...] + gather2[y]

        entering = entering_s[...]
        ahead = jnp.zeros((1, channels), F32)
        for m in range(group):
            back_s[m] = jnp.exp(ahead) * entering + group_prefix[m]
            ahead = ahead + totals1[m]
        far = sorted(range(1, group), key=lambda i: -min((i + 1) // 2, (group - i) // 2 + 1))
        for i in far:
            copy_e(i).start()
        gather3[me_q] = back_s[me_j]

    lax.fori_loop(cuts[1], cuts[2], inside, 0)

    for q in range(group // 2):

        @pl.when(owner(q) != me_j)
        def _():
            pltpu.make_async_remote_copy(
                back_s.at[0], gather3.at[q], se_send.at[0], se_recv.at[q],
                device_id=at_group(owner(q)), device_id_type=MESH,
            ).wait_recv()

    incoming = jnp.concatenate([gather3[q] for q in range(group // 2)], axis=0)
    ones = jnp.ones((8, BLOCK), BF16)
    for k in range(blocks):
        rows = slice(BLOCK * k, BLOCK * (k + 1))
        at_start = starts[k] + jnp.exp(prefix_s[k : k + 1, :]) * incoming
        high, low = split2(at_start)
        read = dot(c2_s[rows, :], jnp.concatenate([high, low], axis=0))
        gated = base_s[rows, :] + slope_s[rows, :] * read
        base_s[rows, :] = gated
        square = gated * gated
        partial = square[:, :LANES]
        for t in range(1, tiles):
            partial = partial + square[:, LANES * t : LANES * (t + 1)]
        high, low = split2(partial)
        row = dot(ones, jnp.concatenate([high, low], axis=1), ((1,), (1,)))
        squares_s[k : k + 1, :] = row[0:1, :]

    def copy_f(z):
        return pltpu.make_async_remote_copy(
            squares_s, gather_sq.at[me_z], sf_send.at[z], sf_recv.at[me_z],
            device_id=(me, z), device_id_type=MESH,
        )

    for z in range(nchan):

        @pl.when(z < me_z)
        def _():
            copy_f(z).start()

    @pl.when(me_z < nchan - 1)
    def _():
        pl.semaphore_wait(z_in, nchan - 1 - me_z)

    for z in range(nchan):

        @pl.when(z > me_z)
        def _():
            copy_f(z).start()

    gather_sq[me_z] = squares_s[...]
    for k in range(blocks):
        rows = slice(BLOCK * k, BLOCK * (k + 1))
        base_s[rows, :] = base_s[rows, :] * gain_s[...]

    for z in range(nchan):

        @pl.when(z != me_z)
        def _():
            pltpu.make_async_remote_copy(
                squares_s, gather_sq.at[z], sf_send.at[z], sf_recv.at[z],
                device_id=(me, z), device_id_type=MESH,
            ).wait_recv()

    total = gather_sq[0]
    for z in range(1, nchan):
        total = total + gather_sq[z]
    factor = jnp.transpose(lax.rsqrt(total / (channels * nchan) + EPSILON))
    for k in range(blocks):
        rows = slice(BLOCK * k, BLOCK * (k + 1))
        scale = jnp.broadcast_to(factor[:, k : k + 1], (BLOCK, LANES))
        for t in range(tiles):
            lanes = slice(LANES * t, LANES * (t + 1))
            out_ref[rows, lanes] = (base_s[rows, lanes] * scale).astype(BF16)

    for i in range(group // 2):

        @pl.when((i != 0) | jnp.logical_not(is_owner))
        def _():
            copy_a(i).wait_send()
            copy_b(i).wait_send()

    @pl.when(is_owner)
    def _():
        for i in range(1, rows_y):

            @pl.when(me_y + i < rows_y)
            def _():
                copy_c(i).wait_send()
                copy_d(i).wait_send()

        for i in range(1, group):
            copy_e(i).wait_send()

    for z in range(nchan):

        @pl.when(z != me_z)
        def _():
            copy_f(z).wait_send()


def per_device(group, rows_y, nchan, x, gate, b, c, step, keep, skip, gain):
    tokens, channels = x.shape
    nstate = b.shape[1]
    heads = step.shape[0]
    blocks = tokens // BLOCK
    owners = group // 2
    piece = nstate // owners
    vmem = pltpu.VMEM
    dma = pltpu.SemaphoreType.DMA
    anywhere = pl.BlockSpec(memory_space=pl.ANY)
    operands = (x, gate, b.T, c.T, step, keep, skip.reshape(1, heads), gain.reshape(1, channels))
    scratch = [
        vmem((tokens, channels), BF16), vmem((tokens, channels), BF16),
        vmem((nstate, tokens), BF16), vmem((nstate, tokens), BF16),
        vmem((heads, tokens), F32), vmem((heads, tokens), F32),
        pltpu.SMEM((1, heads), F32), vmem((1, channels), F32),
        vmem((8 * blocks, BLOCK), F32), vmem((8 * blocks, BLOCK), F32),
        vmem((8 * blocks, BLOCK), F32),
        vmem((tokens, 2 * nstate), BF16),
        vmem((blocks, channels), F32), vmem((1, channels), F32),
        vmem((blocks, nstate, channels), F32), vmem((blocks, nstate, channels), F32),
        vmem((blocks, channels), F32),
        vmem((owners, piece, channels), F32), vmem((group, piece, channels), F32),
        vmem((group, 1, channels), F32), vmem((group, piece, channels), F32),
        vmem((piece, channels), F32), vmem((1, channels), F32),
        vmem((rows_y, piece, channels), F32), vmem((rows_y, 1, channels), F32),
        vmem((piece, channels), F32),
        vmem((group, piece, channels), F32), vmem((owners, piece, channels), F32),
        vmem((tokens, channels), F32), vmem((tokens, channels), F32),
        vmem((blocks, BLOCK), F32), vmem((nchan, blocks, BLOCK), F32),
        dma((7,)), dma, pltpu.SemaphoreType.REGULAR, pltpu.SemaphoreType.REGULAR,
        dma((owners,)), dma((group,)), dma((owners,)), dma((group,)),
        dma((rows_y,)), dma((rows_y,)), dma((rows_y,)), dma((rows_y,)),
        dma((group,)), dma((owners,)), dma((nchan,)), dma((nchan,)),
    ]
    return pl.pallas_call(
        functools.partial(layer, group, rows_y, nchan),
        out_shape=jax.ShapeDtypeStruct((tokens, channels), BF16),
        in_specs=[anywhere] * 8,
        out_specs=pl.BlockSpec(memory_space=pltpu.VMEM),
        scratch_shapes=scratch,
        compiler_params=pltpu.CompilerParams(
            collective_id=0, has_side_effects=True, vmem_limit_bytes=24 * 1024 * 1024
        ),
    )(*[pltpu.with_memory_space_constraint(v, pltpu.HBM) for v in operands])


def build(mesh, group):
    rows_y = mesh.shape["seq"] // group
    placed = (
        P("seq", "chan"), P("seq", "chan"), P("seq", None), P("seq", None),
        P("chan", "seq"), P("chan", "seq"), P("chan"), P("chan"),
    )
    return jax.shard_map(
        functools.partial(per_device, group, rows_y, mesh.shape["chan"]),
        mesh=mesh, in_specs=placed, out_specs=P("seq", "chan"), check_vma=False,
    )


def solution(mesh):
    return build(mesh, GROUP)
```

time: 35 us -> 29 us (0.83)
  Pallas kernels: 32.5 us -> 27.9 us
  local copies, waits for them, and re-layouts: 2.26 us -> 0.97 us
    pallas_call x1, Pallas kernels: 32.5 us -> 27.9 us  [per_device(): pl.pallas_call(functools.partial(layer, group, rows_y, nchan), out_shape=...]
    unnamed x1, local copies, waits for them, and re-layouts: 2.26 us -> 0.97 us
where the time goes in v2:
time: 29 us; the launch traced here: 28.9 us
  Pallas kernels  27.9 us (96%)
  local copies, waits for them, and re-layouts  0.97 us (3%)
    pallas_call x1, Pallas kernels, per_device(): pl.pallas_call(functools.partial(layer, group, rows_y, nchan), out_shape=...  27.9 us
    unnamed x1, local copies, waits for them, and re-layouts  0.97 us

profile of v2, /device:TPU:56, one launch (start us, length us, event | category | flops | bytes accessed | tf_op | source)
XLA Modules:
  0.0 28.9 jit_solution(5892409625772306691)
XLA Ops:
  0.0 27.9 %shard_map.82 = bf16[2048,256]{1,0:T(8,128)(2,1)S(1)} custom-call(bf16[2048,256]{1,0:T(8,128)(2,1)} %x_hbm.1, bf16[2048,256]{1,0:T(8,128)(2,1)} %gate_hbm.1, bf16[64,2048]{1,0:T(8,128)(2,1)} %bitcast.4, bf16[64,2048]{1,0:T(8,128)(2,1)} %bitcast.5, f32[4,2048]{1,0:T(4,128)} %step_hbm.1, f32[4,2048]{1,0:T(4,128)} %keep_hbm.1, f32[1,4]{1,0:T(1,128)} %bitcast.7, ...), custom_call_target="tpu_custom_call" | custom-call | tf_op jit(solution)/shard_map/pallas_call | solution.py:490
  27.9 1.0 %copy.10 = bf16[2048,256]{1,0:T(8,128)(2,1)} copy(bf16[2048,256]{1,0:T(8,128)(2,1)S(1)} %shard_map.82) | data formatting | bytes 2097152

commit v3 on v2

v3 whole, which is shorter than its diff:
```python
import functools

import jax
import jax.numpy as jnp
from jax import lax
from jax.experimental import pallas as pl
from jax.experimental.pallas import tpu as pltpu
from jax.sharding import PartitionSpec as P

BLOCK = 256
LANES = 128
EPSILON = 1e-05
GROUP = 8
MESH = pl.DeviceIdType.MESH
F32 = jnp.float32
BF16 = jnp.bfloat16


def split2(v):
    high = v.astype(BF16)
    return high, (v - high.astype(F32)).astype(BF16)


def dot(a, b, contract=((1,), (0,))):
    return lax.dot_general(a, b, (contract, ((), ())), preferred_element_type=F32)


def layer(
    group, rows_y, nchan,
    x_hbm, gate_hbm, b_hbm, c_hbm, step_hbm, keep_hbm, skip_hbm, gain_hbm,
    base_s, total_ref,
    x_s, gate_s, b_s, c_s, keep_step, skip_s, gain_s,
    keep8, step8, coef8, cum8, c2_s,
    totals, device_total, block_state, starts, prefix_s,
    end_s, gather1, totals1, group_prefix, group_total_state, group_total,
    gather2, totals2, entering_s, back_s, gather3,
    slope_s, squares_s, gather_sq,
    load_sem, keep_sem, skip_sem, y_in, z_in,
    sa_send, sa_recv, sb_send, sb_recv, sc_send, sc_recv,
    sd_send, sd_recv, se_send, se_recv, sf_send, sf_recv,
):
    tokens, channels = x_s.shape
    nstate = b_s.shape[0]
    heads = keep_step.shape[1]
    width = channels // heads
    blocks = tokens // BLOCK
    tiles = channels // LANES
    per_tile = heads // tiles
    piece = 2 * nstate // group

    me = lax.axis_index("seq")
    me_z = lax.axis_index("chan")
    me_y = me // group
    me_j = me % group
    is_owner = me_j % 2 == 1
    me_q = me_j // 2

    def owner(q):
        return 2 * q + 1

    def at_group(j):
        return (me_y * group + j, me_z)

    def at_y(y):
        return (y * group + me_j, me_z)

    def arrived(ref, semaphore):
        pltpu.make_async_remote_copy(
            ref, ref, semaphore, semaphore,
            device_id=(me, (me_z + 1) % nchan), device_id_type=MESH,
        ).wait_recv()

    def sent(ref, semaphore):
        pltpu.make_async_remote_copy(
            ref, ref, semaphore, semaphore,
            device_id=(me, (me_z + 1) % nchan), device_id_type=MESH,
        ).wait_send()

    def rank(y):
        return jnp.minimum(y, rows_y - y) * rows_y + y

    first = [
        pltpu.make_async_copy(keep_hbm, keep_step.at[0], keep_sem),
        pltpu.make_async_copy(step_hbm, keep_step.at[1], keep_sem),
        pltpu.make_async_copy(b_hbm, b_s, load_sem.at[0]),
        pltpu.make_async_copy(x_hbm, x_s, load_sem.at[1]),
    ]
    second = [
        pltpu.make_async_copy(c_hbm, c_s, load_sem.at[2]),
        pltpu.make_async_copy(gate_hbm, gate_s, load_sem.at[3]),
        pltpu.make_async_copy(gain_hbm, gain_s, load_sem.at[4]),
        pltpu.make_async_copy(skip_hbm, skip_s, skip_sem),
    ]
    for copy in first:
        copy.start()

    barrier = pltpu.get_barrier_semaphore()

    def greet(device):
        pl.semaphore_signal(barrier, inc=1, device_id=device, device_id_type=MESH)

    def report(semaphore, device):
        pl.semaphore_signal(semaphore, inc=1, device_id=device, device_id_type=MESH)

    for j in range(group):

        @pl.when((j != me_j) & (is_owner | (j % 2 == 1)))
        def _():
            greet(at_group(j))

    for y in range(rows_y):

        @pl.when(is_owner & (rank(me_y) < rank(y)))
        def _():
            greet(at_y(y))

    for z in range(nchan):

        @pl.when(me_z < z)
        def _():
            greet((me, z))

    lane = lax.broadcasted_iota(jnp.int32, (8, channels), 1)
    row8 = lax.broadcasted_iota(jnp.int32, (8, channels), 0)
    own_head = (lane // width) == row8
    half = lax.broadcasted_iota(jnp.int32, (1, LANES), 1) < width
    past = lax.broadcasted_iota(jnp.int32, (BLOCK, BLOCK), 0)
    here = lax.broadcasted_iota(jnp.int32, (BLOCK, BLOCK), 1)
    upper = jnp.where(past <= here, 1.0, 0.0).astype(BF16)
    later = jnp.where(past > here, 1.0, 0.0).astype(BF16)

    pltpu.make_async_copy(keep_step, keep_step, keep_sem).wait()
    for copy in second:
        copy.start()
    keep8[...] = jnp.zeros_like(keep8)
    step8[...] = jnp.zeros_like(step8)
    for k in range(blocks):
        keep8[8 * k : 8 * k + heads, :] = keep_step[0, :, BLOCK * k : BLOCK * (k + 1)]
        step8[8 * k : 8 * k + heads, :] = keep_step[1, :, BLOCK * k : BLOCK * (k + 1)]
    keep = keep8[...]
    k_high = keep.astype(BF16)
    k_mid, k_low = split2(keep - k_high.astype(F32))
    after = dot(k_high, later) + (dot(k_mid, later) + dot(k_low, later))
    coef8[...] = jnp.exp(after) * step8[...]

    first[2].wait()
    first[3].wait()
    cum8[...] = dot(k_high, upper) + (dot(k_mid, upper) + dot(k_low, upper))
    for k in range(blocks):
        coef = coef8[8 * k : 8 * k + 8, :]
        bt = b_s[:, BLOCK * k : BLOCK * (k + 1)].astype(F32)
        for t in range(tiles):
            lines = jnp.concatenate(
                [(bt * coef[h : h + 1, :]).astype(BF16) for h in (2 * t, 2 * t + 1)], axis=0
            )
            both = dot(lines, x_s[BLOCK * k : BLOCK * (k + 1), LANES * t : LANES * (t + 1)])
            block_state[k, :, LANES * t : LANES * (t + 1)] = jnp.where(
                half, both[:nstate], both[nstate:]
            )
    for k in range(blocks):
        last = cum8[8 * k : 8 * k + 8, BLOCK - 1 : BLOCK]
        spread = jnp.where(own_head, jnp.broadcast_to(last, (8, channels)), 0.0)
        totals[k : k + 1, :] = jnp.sum(spread, axis=0, keepdims=True)
    device_total[...] = jnp.sum(totals[...], axis=0, keepdims=True)
    running = jnp.zeros((nstate, channels), F32)
    for k in range(blocks):
        starts[k] = running
        running = jnp.exp(totals[k : k + 1, :]) * running + block_state[k]
    for q in range(group // 2):
        end_s[q] = running[piece * q : piece * (q + 1), :]

    greeted = me_z + jnp.where(is_owner, group - 1, group // 2)
    expected_y = 0
    for y in range(rows_y):
        greeted = greeted + jnp.where(is_owner & (rank(y) < rank(me_y)), 1, 0)
        expected_y = expected_y + jnp.where((y > me_y) & (rank(y) > rank(me_y)), 1, 0)
    pl.semaphore_wait(barrier, greeted)

    def copy_a(i):
        return pltpu.make_async_remote_copy(
            device_total, totals1.at[me_j], sa_send, sa_recv,
            device_id=at_group(owner((me_q + i) % (group // 2))), device_id_type=MESH,
        )

    def copy_b(i):
        q = (me_q + i) % (group // 2)
        return pltpu.make_async_remote_copy(
            end_s.at[q], gather1.at[me_j], sb_send, sb_recv,
            device_id=at_group(owner(q)), device_id_type=MESH,
        )

    others = [group // 4] + [i for i in range(group // 2) if i != group // 4]
    for i in others:

        @pl.when((i != 0) | jnp.logical_not(is_owner))
        def _():
            copy_a(i).start()
            copy_b(i).start()

    for y in range(rows_y):

        @pl.when(is_owner & (y < me_y) & (rank(y) < rank(me_y)))
        def _():
            report(y_in, at_y(y))

    for z in range(nchan):

        @pl.when(z < me_z)
        def _():
            report(z_in, (me, z))

    @pl.when(is_owner)
    def _():
        gather1[me_j] = end_s[me_q]
        totals1[me_j] = device_total[...]

    before = jnp.zeros((1, channels), F32)
    for k in range(blocks):
        prefix_s[k : k + 1, :] = before
        before = before + totals[k : k + 1, :]

    for copy in second:
        copy.wait()
    head_of = lax.broadcasted_iota(jnp.int32, (1, channels), 1) // width
    skip_row = jnp.zeros((1, channels), F32)
    for h in range(heads):
        skip_row = jnp.where(head_of == h, skip_s[0, h], skip_row)
    diagonal = (
        lax.broadcasted_iota(jnp.int32, (LANES, LANES), 0)
        >= lax.broadcasted_iota(jnp.int32, (LANES, LANES), 1)
    )

    def inside(k, carry):
        rows = pl.ds(pl.multiple_of(k * BLOCK, BLOCK), BLOCK)
        slab_at = pl.ds(pl.multiple_of(k * 8, 8), 8)
        slab = cum8[slab_at, :]
        steps = step8[slab_at, :]
        columns = jnp.transpose(slab)
        c_block = c_s[:, rows]
        c_pair = jnp.transpose(jnp.concatenate([c_block, c_block], axis=0))
        c2_s[rows, :] = c_pair
        scores = dot(c_pair[:, :nstate], b_s[:, rows])
        high, low = split2(starts[k])
        read = dot(c_pair, jnp.concatenate([high, low], axis=0))
        carried = jnp.exp(prefix_s[pl.ds(k, 1), :])
        for t in range(tiles):
            lanes = slice(LANES * t, LANES * (t + 1))
            weights, spreads = [], []
            for h in (2 * t, 2 * t + 1):
                column = jnp.broadcast_to(columns[:, h : h + 1], (BLOCK, LANES))
                spreads.append(column)

                def weight(r, s):
                    rr, ss = slice(LANES * r, LANES * (r + 1)), slice(LANES * s, LANES * (s + 1))
                    w = (
                        scores[rr, ss]
                        * jnp.exp(column[rr, :] - slab[h : h + 1, ss])
                        * steps[h : h + 1, ss]
                    )
                    return (jnp.where(diagonal, w, 0.0) if r == s else w).astype(BF16)

                top = jnp.concatenate([weight(0, 0), jnp.zeros((LANES, LANES), BF16)], axis=1)
                bottom = jnp.concatenate([weight(1, 0), weight(1, 1)], axis=1)
                weights += [top, bottom]
            x_tile = x_s[rows, lanes]
            both = dot(jnp.concatenate(weights, axis=0), x_tile)
            value = jnp.where(half, both[:BLOCK], both[BLOCK:])
            value = value + skip_row[:, lanes] * x_tile.astype(F32)
            gate = gate_s[rows, lanes].astype(F32)
            gate = gate / (1.0 + jnp.exp(-gate))
            slope = jnp.exp(jnp.where(half, spreads[0], spreads[1])) * gate
            base_s[rows, lanes] = value * gate + slope * read[:, lanes]
            slope_s[rows, lanes] = slope * carried[:, lanes]
        return carry

    third = (blocks * 3) // 8
    middle = jnp.where(me_y > 0, third + blocks // 4, third)
    lax.fori_loop(0, third, inside, 0)

    def copy_c(i):
        return pltpu.make_async_remote_copy(
            group_total, totals2.at[me_y], sc_send, sc_recv,
            device_id=at_y(me_y + i), device_id_type=MESH,
        )

    def copy_d(i):
        return pltpu.make_async_remote_copy(
            group_total_state, gather2.at[me_y], sd_send, sd_recv,
            device_id=at_y(me_y + i), device_id_type=MESH,
        )

    @pl.when(is_owner)
    def _():
        @pl.when(expected_y > 0)
        def _():
            pl.semaphore_wait(y_in, expected_y)

        arrived(totals1.at[pl.ds(0, group - 1)], sa_recv)
        total = totals1[0]
        for m in range(1, group):
            total = total + totals1[m]
        group_total[...] = total
        for i in range(1, rows_y):

            @pl.when(me_y + i < rows_y)
            def _():
                copy_c(i).start()

        arrived(gather1.at[pl.ds(0, group - 1)], sb_recv)
        state = jnp.zeros((piece, channels), F32)
        for m in range(group):
            group_prefix[m] = state
            state = jnp.exp(totals1[m]) * state + gather1[m]
        group_total_state[...] = state
        for i in sorted(range(1, rows_y), key=lambda i: -min(i, rows_y - i)):

            @pl.when(me_y + i < rows_y)
            def _():
                copy_d(i).start()


    def copy_e(i):
        p = (me_j + i) % group
        return pltpu.make_async_remote_copy(
            back_s.at[p], gather3.at[me_q], se_send, se_recv,
            device_id=at_group(p), device_id_type=MESH,
        )

    lax.fori_loop(third, middle, inside, 0)

    @pl.when(is_owner)
    def _():
        entering_s[...] = jnp.zeros_like(entering_s)
        for n in range(1, rows_y):

            @pl.when(me_y == n)
            def _():
                arrived(totals2.at[pl.ds(0, n)], sc_recv)
                arrived(gather2.at[pl.ds(0, n)], sd_recv)
                state = gather2[0]
                for y in range(1, n):
                    state = jnp.exp(totals2[y]) * state + gather2[y]
                entering_s[...] = state

        entering = entering_s[...]
        ahead = jnp.zeros((1, channels), F32)
        for m in range(group):
            back_s[m] = jnp.exp(ahead) * entering + group_prefix[m]
            ahead = ahead + totals1[m]
        for i in sorted(range(1, group), key=lambda i: i % 2 - 2 * min((i + 1) // 2, (group - i) // 2) - 3 * (i % 2)):
            copy_e(i).start()
        gather3[me_q] = back_s[me_j]

    lax.fori_loop(middle, blocks, inside, 0)

    @pl.when(is_owner)
    def _():
        arrived(gather3.at[pl.ds(0, group // 2 - 1)], se_recv)

    @pl.when(jnp.logical_not(is_owner))
    def _():
        arrived(gather3, se_recv)

    high, low = split2(jnp.concatenate([gather3[q] for q in range(group // 2)], axis=0))
    incoming = jnp.concatenate([high, low], axis=0)
    sums = jnp.zeros((BLOCK, LANES), F32)
    place = lax.broadcasted_iota(jnp.int32, (BLOCK, LANES), 1)
    for k in range(blocks):
        rows = slice(BLOCK * k, BLOCK * (k + 1))
        read = dot(c2_s[rows, :], incoming)
        gated = base_s[rows, :] + slope_s[rows, :] * read
        base_s[rows, :] = gated
        square = gated * gated
        partial = square[:, :LANES]
        for t in range(1, tiles):
            partial = partial + square[:, LANES * t : LANES * (t + 1)]
        sums = jnp.where(place == k, jnp.sum(partial, axis=1, keepdims=True), sums)
    squares_s[...] = jnp.transpose(sums)[:blocks, :]

    def copy_f(z):
        return pltpu.make_async_remote_copy(
            squares_s, gather_sq.at[me_z], sf_send, sf_recv,
            device_id=(me, z), device_id_type=MESH,
        )

    for z in range(nchan):

        @pl.when(z < me_z)
        def _():
            copy_f(z).start()

    @pl.when(me_z < nchan - 1)
    def _():
        pl.semaphore_wait(z_in, nchan - 1 - me_z)

    for z in range(nchan):

        @pl.when(z > me_z)
        def _():
            copy_f(z).start()

    gather_sq[me_z] = squares_s[...]
    for k in range(blocks):
        rows = slice(BLOCK * k, BLOCK * (k + 1))
        base_s[rows, :] = base_s[rows, :] * gain_s[...]

    arrived(gather_sq.at[pl.ds(0, nchan - 1)], sf_recv)

    total = gather_sq[0]
    for z in range(1, nchan):
        total = total + gather_sq[z]
    total_ref[...] = total

    @pl.when(is_owner)
    def _():
        sent(totals1.at[pl.ds(0, group // 2 - 1)], sa_send)
        sent(end_s.at[pl.ds(0, group // 2 - 1)], sb_send)
        sent(back_s.at[pl.ds(0, group - 1)], se_send)
        for n in range(1, rows_y):

            @pl.when(me_y == rows_y - 1 - n)
            def _():
                sent(totals2.at[pl.ds(0, n)], sc_send)
                sent(gather2.at[pl.ds(0, n)], sd_send)

    @pl.when(jnp.logical_not(is_owner))
    def _():
        sent(totals1.at[pl.ds(0, group // 2)], sa_send)
        sent(end_s, sb_send)

    sent(gather_sq.at[pl.ds(0, nchan - 1)], sf_send)


def scale_rows(width, base_ref, total_ref, out_hbm, out_s, store_sem):
    tokens, channels = base_ref.shape
    blocks = tokens // BLOCK
    factor = lax.rsqrt(total_ref[...] / width + EPSILON)
    stores = []
    for k in range(blocks):
        for r in range(BLOCK // LANES):
            rows = slice(BLOCK * k + LANES * r, BLOCK * k + LANES * (r + 1))
            line = factor[k : k + 1, LANES * r : LANES * (r + 1)]
            scale = jnp.transpose(jnp.broadcast_to(line, (LANES, LANES)))
            for t in range(channels // LANES):
                lanes = slice(LANES * t, LANES * (t + 1))
                out_s[rows, lanes] = (base_ref[rows, lanes] * scale).astype(BF16)
        rows = slice(BLOCK * k, BLOCK * (k + 1))
        store = pltpu.make_async_copy(out_s.at[rows, :], out_hbm.at[rows, :], store_sem.at[k])
        store.start()
        stores.append(store)
    for store in stores:
        store.wait()


def per_device(group, rows_y, nchan, x, gate, b, c, step, keep, skip, gain):
    tokens, channels = x.shape
    nstate = b.shape[1]
    heads = step.shape[0]
    blocks = tokens // BLOCK
    owners = group // 2
    piece = nstate // owners
    vmem = pltpu.VMEM
    dma = pltpu.SemaphoreType.DMA
    anywhere = pl.BlockSpec(memory_space=pl.ANY)
    operands = (x, gate, b.T, c.T, step, keep, skip.reshape(1, heads), gain.reshape(1, channels))
    scratch = [
        vmem((tokens, channels), BF16), vmem((tokens, channels), BF16),
        vmem((nstate, tokens), BF16), vmem((nstate, tokens), BF16),
        vmem((2, heads, tokens), F32),
        pltpu.SMEM((1, heads), F32), vmem((1, channels), F32),
        vmem((8 * blocks, BLOCK), F32), vmem((8 * blocks, BLOCK), F32),
        vmem((8 * blocks, BLOCK), F32), vmem((8 * blocks, BLOCK), F32),
        vmem((tokens, 2 * nstate), BF16),
        vmem((blocks, channels), F32), vmem((1, channels), F32),
        vmem((blocks, nstate, channels), F32), vmem((blocks, nstate, channels), F32),
        vmem((blocks, channels), F32),
        vmem((owners, piece, channels), F32), vmem((group, piece, channels), F32),
        vmem((group, 1, channels), F32), vmem((group, piece, channels), F32),
        vmem((piece, channels), F32), vmem((1, channels), F32),
        vmem((rows_y, piece, channels), F32), vmem((rows_y, 1, channels), F32),
        vmem((piece, channels), F32),
        vmem((group, piece, channels), F32), vmem((owners, piece, channels), F32),
        vmem((tokens, channels), F32),
        vmem((blocks, BLOCK), F32), vmem((nchan, blocks, BLOCK), F32),
        dma((5,)), dma, dma, pltpu.SemaphoreType.REGULAR, pltpu.SemaphoreType.REGULAR,
    ] + [dma] * 12
    base, total = pl.pallas_call(
        functools.partial(layer, group, rows_y, nchan),
        out_shape=(
            jax.ShapeDtypeStruct((tokens, channels), F32),
            jax.ShapeDtypeStruct((blocks, BLOCK), F32),
        ),
        in_specs=[anywhere] * 8,
        out_specs=(pl.BlockSpec(memory_space=pltpu.VMEM),) * 2,
        scratch_shapes=scratch,
        compiler_params=pltpu.CompilerParams(
            collective_id=0, has_side_effects=True, vmem_limit_bytes=24 * 1024 * 1024
        ),
    )(*[pltpu.with_memory_space_constraint(v, pltpu.HBM) for v in operands])
    return pl.pallas_call(
        functools.partial(scale_rows, channels * nchan),
        out_shape=jax.ShapeDtypeStruct((tokens, channels), BF16),
        in_specs=[pl.BlockSpec(memory_space=pltpu.VMEM)] * 2,
        out_specs=anywhere,
        scratch_shapes=[vmem((tokens, channels), BF16), dma((blocks,))],
        compiler_params=pltpu.CompilerParams(vmem_limit_bytes=8 * 1024 * 1024),
    )(base, total)


def build(mesh, group):
    rows_y = mesh.shape["seq"] // group
    placed = (
        P("seq", "chan"), P("seq", "chan"), P("seq", None), P("seq", None),
        P("chan", "seq"), P("chan", "seq"), P("chan"), P("chan"),
    )
    return jax.shard_map(
        functools.partial(per_device, group, rows_y, mesh.shape["chan"]),
        mesh=mesh, in_specs=placed, out_specs=P("seq", "chan"), check_vma=False,
    )


def solution(mesh):
    return build(mesh, GROUP)
```

time: 29 us -> 27.5 us (0.948)
  local copies, waits for them, and re-layouts: 0.97 us -> 0 us
  Pallas kernels: 27.9 us -> 27.3 us
    pallas_call x1, Pallas kernels: 27.9 us -> 26.2 us  [per_device(): pl.pallas_call(functools.partial(layer, group, rows_y, nchan), out_shape=...]
    pallas_call x0 -> x1, Pallas kernels: none -> 1.14 us  [per_device(): pl.pallas_call(functools.partial(scale_rows, channels * nchan), out_shape...]
    unnamed x1 -> x0, local copies, waits for them, and re-layouts: 0.97 us -> none
where the time goes in v3:
time: 27.5 us; the launch traced here: 27.3 us
  Pallas kernels  27.3 us (99%)
    pallas_call x1, Pallas kernels, per_device(): pl.pallas_call(functools.partial(layer, group, rows_y, nchan), out_shape=...  26.2 us
    pallas_call x1, Pallas kernels, per_device(): pl.pallas_call(functools.partial(scale_rows, channels * nchan), out_shape...  1.14 us

profile of v3, /device:TPU:56, one launch (start us, length us, event | category | flops | bytes accessed | tf_op | source)
XLA Modules:
  0.0 27.3 jit_solution(5779257338941377592)
XLA Ops:
  0.0 26.2 %shard_map.82 = (f32[2048,256]{1,0:T(8,128)S(1)}, f32[8,256]{1,0:T(8,128)S(1)}) custom-call(bf16[2048,256]{1,0:T(8,128)(2,1)} %x_hbm.1, bf16[2048,256]{1,0:T(8,128)(2,1)} %gate_hbm.1, bf16[64,2048]{1,0:T(8,128)(2,1)} %bitcast.4, bf16[64,2048]{1,0:T(8,128)(2,1)} %bitcast.5, f32[4,2048]{1,0:T(4,128)} %step_hbm.1, f32[4,2048]{1,0:T(4,128)} %keep_hbm.1, ...), custom_call_target="tpu_custom_call" | custom-call | tf_op jit(solution)/shard_map/pallas_call | solution.py:487
  26.2 1.1 %shard_map.83 = bf16[2048,256]{1,0:T(8,128)(2,1)} custom-call(f32[2048,256]{1,0:T(8,128)S(1)} %get-tuple-element.7.base_ref, f32[8,256]{1,0:T(8,128)S(1)} %get-tuple-element.8.total_ref), custom_call_target="tpu_custom_call" | custom-call | tf_op jit(solution)/shard_map/pallas_call | solution.py:500

commit v4 on v3

--- a/solution.py
+++ b/solution.py
@@ -34,10 +34,9 @@
     totals, device_total, block_state, starts, prefix_s,
     end_s, gather1, totals1, group_prefix, group_total_state, group_total,
     gather2, totals2, entering_s, back_s, gather3,
-    slope_s, squares_s, gather_sq,
+    slope_s, squares_s, gather_sq, lines_s,
     load_sem, keep_sem, skip_sem, y_in, z_in,
-    sa_send, sa_recv, sb_send, sb_recv, sc_send, sc_recv,
-    sd_send, sd_recv, se_send, se_recv, sf_send, sf_recv,
+    send_sem, b_recv, d_recv, e_recv, f_recv,
 ):
     tokens, channels = x_s.shape
     nstate = b_s.shape[0]
@@ -64,17 +63,20 @@
     def at_y(y):
         return (y * group + me_j, me_z)
 
-    def arrived(ref, semaphore):
-        pltpu.make_async_remote_copy(
+    def lines_of(count, semaphore):
+        ref = lines_s.at[pl.ds(0, count)]
+        return pltpu.make_async_remote_copy(
             ref, ref, semaphore, semaphore,
             device_id=(me, (me_z + 1) % nchan), device_id_type=MESH,
-        ).wait_recv()
-
-    def sent(ref, semaphore):
-        pltpu.make_async_remote_copy(
-            ref, ref, semaphore, semaphore,
-            device_id=(me, (me_z + 1) % nchan), device_id_type=MESH,
-        ).wait_send()
+        )
+
+    def arrived(count, semaphore):
+        lines_of(count, semaphore).wait_recv()
+
+    def sent(count):
+        lines_of(count, send_sem).wait_send()
+
+    owners = group // 2
 
     def rank(y):
         return jnp.minimum(y, rows_y - y) * rows_y + y
@@ -178,14 +180,14 @@
 
     def copy_a(i):
         return pltpu.make_async_remote_copy(
-            device_total, totals1.at[me_j], sa_send, sa_recv,
+            device_total, totals1.at[me_j], send_sem, b_recv,
             device_id=at_group(owner((me_q + i) % (group // 2))), device_id_type=MESH,
         )
 
     def copy_b(i):
         q = (me_q + i) % (group // 2)
         return pltpu.make_async_remote_copy(
-            end_s.at[q], gather1.at[me_j], sb_send, sb_recv,
+            end_s.at[q], gather1.at[me_j], send_sem, b_recv,
             device_id=at_group(owner(q)), device_id_type=MESH,
         )
 
@@ -279,13 +281,13 @@
 
     def copy_c(i):
         return pltpu.make_async_remote_copy(
-            group_total, totals2.at[me_y], sc_send, sc_recv,
+            group_total, totals2.at[me_y], send_sem, d_recv,
             device_id=at_y(me_y + i), device_id_type=MESH,
         )
 
     def copy_d(i):
         return pltpu.make_async_remote_copy(
-            group_total_state, gather2.at[me_y], sd_send, sd_recv,
+            group_total_state, gather2.at[me_y], send_sem, d_recv,
             device_id=at_y(me_y + i), device_id_type=MESH,
         )
 
@@ -295,7 +297,7 @@
         def _():
             pl.semaphore_wait(y_in, expected_y)
 
-        arrived(totals1.at[pl.ds(0, group - 1)], sa_recv)
+        arrived((group - 1) * (piece + 1), b_recv)
         total = totals1[0]
         for m in range(1, group):
             total = total + totals1[m]
@@ -306,7 +308,6 @@
             def _():
                 copy_c(i).start()
 
-        arrived(gather1.at[pl.ds(0, group - 1)], sb_recv)
         state = jnp.zeros((piece, channels), F32)
         for m in range(group):
             group_prefix[m] = state
@@ -322,7 +323,7 @@
     def copy_e(i):
         p = (me_j + i) % group
         return pltpu.make_async_remote_copy(
-            back_s.at[p], gather3.at[me_q], se_send, se_recv,
+            back_s.at[p], gather3.at[me_q], send_sem, e_recv,
             device_id=at_group(p), device_id_type=MESH,
         )
 
@@ -335,8 +336,7 @@
 
             @pl.when(me_y == n)
             def _():
-                arrived(totals2.at[pl.ds(0, n)], sc_recv)
-                arrived(gather2.at[pl.ds(0, n)], sd_recv)
+                arrived(n * (piece + 1), d_recv)
                 state = gather2[0]
                 for y in range(1, n):
                     state = jnp.exp(totals2[y]) * state + gather2[y]
@@ -355,11 +355,11 @@
 
     @pl.when(is_owner)
     def _():
-        arrived(gather3.at[pl.ds(0, group // 2 - 1)], se_recv)
+        arrived((owners - 1) * piece, e_recv)
 
     @pl.when(jnp.logical_not(is_owner))
     def _():
-        arrived(gather3, se_recv)
+        arrived(owners * piece, e_recv)
 
     high, low = split2(jnp.concatenate([gather3[q] for q in range(group // 2)], axis=0))
     incoming = jnp.concatenate([high, low], axis=0)
@@ -379,7 +379,7 @@
 
     def copy_f(z):
         return pltpu.make_async_remote_copy(
-            squares_s, gather_sq.at[me_z], sf_send, sf_recv,
+            squares_s, gather_sq.at[me_z], send_sem, f_recv,
             device_id=(me, z), device_id_type=MESH,
         )
 
@@ -404,52 +404,39 @@
         rows = slice(BLOCK * k, BLOCK * (k + 1))
         base_s[rows, :] = base_s[rows, :] * gain_s[...]
 
-    arrived(gather_sq.at[pl.ds(0, nchan - 1)], sf_recv)
+    arrived((nchan - 1) * blocks, f_recv)
 
     total = gather_sq[0]
     for z in range(1, nchan):
         total = total + gather_sq[z]
     total_ref[...] = total
 
-    @pl.when(is_owner)
-    def _():
-        sent(totals1.at[pl.ds(0, group // 2 - 1)], sa_send)
-        sent(end_s.at[pl.ds(0, group // 2 - 1)], sb_send)
-        sent(back_s.at[pl.ds(0, group - 1)], se_send)
-        for n in range(1, rows_y):
-
-            @pl.when(me_y == rows_y - 1 - n)
-            def _():
-                sent(totals2.at[pl.ds(0, n)], sc_send)
-                sent(gather2.at[pl.ds(0, n)], sd_send)
+    for n in range(rows_y):
+
+        @pl.when(is_owner & (me_y == rows_y - 1 - n))
+        def _():
+            sent((owners - 1 + n) * (piece + 1) + (group - 1) * piece + (nchan - 1) * blocks)
 
     @pl.when(jnp.logical_not(is_owner))
     def _():
-        sent(totals1.at[pl.ds(0, group // 2)], sa_send)
-        sent(end_s, sb_send)
-
-    sent(gather_sq.at[pl.ds(0, nchan - 1)], sf_send)
+        sent(owners * (piece + 1) + (nchan - 1) * blocks)
 
 
 def scale_rows(width, base_ref, total_ref, out_hbm, out_s, store_sem):
     tokens, channels = base_ref.shape
     blocks = tokens // BLOCK
     factor = lax.rsqrt(total_ref[...] / width + EPSILON)
-    stores = []
     for k in range(blocks):
         for r in range(BLOCK // LANES):
+            part = slice(LANES * r, LANES * (r + 1))
             rows = slice(BLOCK * k + LANES * r, BLOCK * k + LANES * (r + 1))
-            line = factor[k : k + 1, LANES * r : LANES * (r + 1)]
-            scale = jnp.transpose(jnp.broadcast_to(line, (LANES, LANES)))
+            scale = jnp.transpose(jnp.broadcast_to(factor[k : k + 1, part], (LANES, LANES)))
             for t in range(channels // LANES):
                 lanes = slice(LANES * t, LANES * (t + 1))
                 out_s[rows, lanes] = (base_ref[rows, lanes] * scale).astype(BF16)
         rows = slice(BLOCK * k, BLOCK * (k + 1))
-        store = pltpu.make_async_copy(out_s.at[rows, :], out_hbm.at[rows, :], store_sem.at[k])
-        store.start()
-        stores.append(store)
-    for store in stores:
-        store.wait()
+        pltpu.make_async_copy(out_s.at[rows, :], out_hbm.at[rows, :], store_sem).start()
+    pltpu.make_async_copy(out_s, out_hbm, store_sem).wait()
 
 
 def per_device(group, rows_y, nchan, x, gate, b, c, step, keep, skip, gain):
@@ -482,8 +469,9 @@
         vmem((group, piece, channels), F32), vmem((owners, piece, channels), F32),
         vmem((tokens, channels), F32),
         vmem((blocks, BLOCK), F32), vmem((nchan, blocks, BLOCK), F32),
+        vmem(((owners + rows_y) * (piece + 1) + group * piece + nchan * blocks, 1, channels), F32),
         dma((5,)), dma, dma, pltpu.SemaphoreType.REGULAR, pltpu.SemaphoreType.REGULAR,
-    ] + [dma] * 12
+    ] + [dma] * 5
     base, total = pl.pallas_call(
         functools.partial(layer, group, rows_y, nchan),
         out_shape=(
@@ -502,7 +490,7 @@
         out_shape=jax.ShapeDtypeStruct((tokens, channels), BF16),
         in_specs=[pl.BlockSpec(memory_space=pltpu.VMEM)] * 2,
         out_specs=anywhere,
-        scratch_shapes=[vmem((tokens, channels), BF16), dma((blocks,))],
+        scratch_shapes=[vmem((tokens, channels), BF16), dma],
         compiler_params=pltpu.CompilerParams(vmem_limit_bytes=8 * 1024 * 1024),
     )(base, total)
 

time: 27.5 us -> 27.4 us (level)
  no operation moved by 1% of the time
where the time goes in v4:
time: 27.4 us; the launch traced here: 27.2 us
  Pallas kernels  27.2 us (99%)
    pallas_call x1, Pallas kernels, per_device(): pl.pallas_call(functools.partial(layer, group, rows_y, nchan), out_shape=...  26.1 us
    pallas_call x1, Pallas kernels, per_device(): pl.pallas_call(functools.partial(scale_rows, channels * nchan), out_shape...  1.08 us

profile of v4, /device:TPU:56, one launch (start us, length us, event | category | flops | bytes accessed | tf_op | source)
XLA Modules:
  0.0 27.2 jit_solution(2960641032161697068)
XLA Ops:
  0.0 26.1 %shard_map.82 = (f32[2048,256]{1,0:T(8,128)S(1)}, f32[8,256]{1,0:T(8,128)S(1)}) custom-call(bf16[2048,256]{1,0:T(8,128)(2,1)} %x_hbm.1, bf16[2048,256]{1,0:T(8,128)(2,1)} %gate_hbm.1, bf16[64,2048]{1,0:T(8,128)(2,1)} %bitcast.4, bf16[64,2048]{1,0:T(8,128)(2,1)} %bitcast.5, f32[4,2048]{1,0:T(4,128)} %step_hbm.1, f32[4,2048]{1,0:T(4,128)} %keep_hbm.1, ...), custom_call_target="tpu_custom_call" | custom-call | tf_op jit(solution)/shard_map/pallas_call | solution.py:475
  26.1 1.1 %shard_map.83 = bf16[2048,256]{1,0:T(8,128)(2,1)} custom-call(f32[2048,256]{1,0:T(8,128)S(1)} %get-tuple-element.7.base_ref, f32[8,256]{1,0:T(8,128)S(1)} %get-tuple-element.8.total_ref), custom_call_target="tpu_custom_call" | custom-call | tf_op jit(solution)/shard_map/pallas_call | solution.py:488

commit v5 on v4

--- a/solution.py
+++ b/solution.py
@@ -81,6 +81,8 @@
     def rank(y):
         return jnp.minimum(y, rows_y - y) * rows_y + y
 
+    by_rank = sorted(range(rows_y), key=lambda y: min(y, rows_y - y) * rows_y + y)
+
     first = [
         pltpu.make_async_copy(keep_hbm, keep_step.at[0], keep_sem),
         pltpu.make_async_copy(step_hbm, keep_step.at[1], keep_sem),
@@ -172,10 +174,8 @@
         end_s[q] = running[piece * q : piece * (q + 1), :]
 
     greeted = me_z + jnp.where(is_owner, group - 1, group // 2)
-    expected_y = 0
     for y in range(rows_y):
         greeted = greeted + jnp.where(is_owner & (rank(y) < rank(me_y)), 1, 0)
-        expected_y = expected_y + jnp.where((y > me_y) & (rank(y) > rank(me_y)), 1, 0)
     pl.semaphore_wait(barrier, greeted)
 
     def copy_a(i):
@@ -203,7 +203,7 @@
 
         @pl.when(is_owner & (y < me_y) & (rank(y) < rank(me_y)))
         def _():
-            report(y_in, at_y(y))
+            report(y_in.at[me_y], at_y(y))
 
     for z in range(nchan):
 
@@ -279,46 +279,40 @@
     middle = jnp.where(me_y > 0, third + blocks // 4, third)
     lax.fori_loop(0, third, inside, 0)
 
-    def copy_c(i):
+    def copy_c(y):
         return pltpu.make_async_remote_copy(
             group_total, totals2.at[me_y], send_sem, d_recv,
-            device_id=at_y(me_y + i), device_id_type=MESH,
-        )
-
-    def copy_d(i):
+            device_id=at_y(y), device_id_type=MESH,
+        )
+
+    def copy_d(y):
         return pltpu.make_async_remote_copy(
             group_total_state, gather2.at[me_y], send_sem, d_recv,
-            device_id=at_y(me_y + i), device_id_type=MESH,
+            device_id=at_y(y), device_id_type=MESH,
         )
 
     @pl.when(is_owner)
     def _():
-        @pl.when(expected_y > 0)
-        def _():
-            pl.semaphore_wait(y_in, expected_y)
-
         arrived((group - 1) * (piece + 1), b_recv)
         total = totals1[0]
         for m in range(1, group):
             total = total + totals1[m]
         group_total[...] = total
-        for i in range(1, rows_y):
-
-            @pl.when(me_y + i < rows_y)
-            def _():
-                copy_c(i).start()
-
         state = jnp.zeros((piece, channels), F32)
         for m in range(group):
             group_prefix[m] = state
             state = jnp.exp(totals1[m]) * state + gather1[m]
         group_total_state[...] = state
-        for i in sorted(range(1, rows_y), key=lambda i: -min(i, rows_y - i)):
-
-            @pl.when(me_y + i < rows_y)
+        for y in by_rank:
+
+            @pl.when((y > me_y) & (rank(me_y) < rank(y)))
             def _():
-                copy_d(i).start()
-
+                pl.semaphore_wait(y_in.at[y], 1)
+
+            @pl.when(y > me_y)
+            def _():
+                copy_c(y).start()
+                copy_d(y).start()
 
     def copy_e(i):
         p = (me_j + i) % group
@@ -470,7 +464,7 @@
         vmem((tokens, channels), F32),
         vmem((blocks, BLOCK), F32), vmem((nchan, blocks, BLOCK), F32),
         vmem(((owners + rows_y) * (piece + 1) + group * piece + nchan * blocks, 1, channels), F32),
-        dma((5,)), dma, dma, pltpu.SemaphoreType.REGULAR, pltpu.SemaphoreType.REGULAR,
+        dma((5,)), dma, dma, pltpu.SemaphoreType.REGULAR((rows_y,)), pltpu.SemaphoreType.REGULAR,
     ] + [dma] * 5
     base, total = pl.pallas_call(
         functools.partial(layer, group, rows_y, nchan),

time: 27.4 us -> 27.2 us (level)
  no operation moved by 1% of the time
where the time goes in v5:
time: 27.2 us; the launch traced here: 27.1 us
  Pallas kernels  27.1 us (100%)
    pallas_call x1, Pallas kernels, per_device(): pl.pallas_call(functools.partial(layer, group, rows_y, nchan), out_shape=...  26 us
    pallas_call x1, Pallas kernels, per_device(): pl.pallas_call(functools.partial(scale_rows, channels * nchan), out_shape...  1.08 us

profile of v5, /device:TPU:56, one launch (start us, length us, event | category | flops | bytes accessed | tf_op | source)
XLA Modules:
  0.0 27.1 jit_solution(6679011492262282357)
XLA Ops:
  0.0 26.0 %shard_map.82 = (f32[2048,256]{1,0:T(8,128)S(1)}, f32[8,256]{1,0:T(8,128)S(1)}) custom-call(bf16[2048,256]{1,0:T(8,128)(2,1)} %x_hbm.1, bf16[2048,256]{1,0:T(8,128)(2,1)} %gate_hbm.1, bf16[64,2048]{1,0:T(8,128)(2,1)} %bitcast.4, bf16[64,2048]{1,0:T(8,128)(2,1)} %bitcast.5, f32[4,2048]{1,0:T(4,128)} %step_hbm.1, f32[4,2048]{1,0:T(4,128)} %keep_hbm.1, ...), custom_call_target="tpu_custom_call" | custom-call | tf_op jit(solution)/shard_map/pallas_call | solution.py:469
  26.0 1.1 %shard_map.83 = bf16[2048,256]{1,0:T(8,128)(2,1)} custom-call(f32[2048,256]{1,0:T(8,128)S(1)} %get-tuple-element.7.base_ref, f32[8,256]{1,0:T(8,128)S(1)} %get-tuple-element.8.total_ref), custom_call_target="tpu_custom_call" | custom-call | tf_op jit(solution)/shard_map/pallas_call | solution.py:482

commit v6 on v5

--- a/solution.py
+++ b/solution.py
@@ -33,7 +33,7 @@
     keep8, step8, coef8, cum8, c2_s,
     totals, device_total, block_state, starts, prefix_s,
     end_s, gather1, totals1, group_prefix, group_total_state, group_total,
-    gather2, totals2, entering_s, back_s, gather3,
+    gather2, totals2, entering_s, decay_s, back_s, gather3,
     slope_s, squares_s, gather_sq, lines_s,
     load_sem, keep_sem, skip_sem, y_in, z_in,
     send_sem, b_recv, d_recv, e_recv, f_recv,
@@ -108,7 +108,7 @@
 
     for j in range(group):
 
-        @pl.when((j != me_j) & (is_owner | (j % 2 == 1)))
+        @pl.when((j != me_j) & is_owner)
         def _():
             greet(at_group(j))
 
@@ -173,7 +173,7 @@
     for q in range(group // 2):
         end_s[q] = running[piece * q : piece * (q + 1), :]
 
-    greeted = me_z + jnp.where(is_owner, group - 1, group // 2)
+    greeted = me_z + jnp.where(is_owner, owners - 1, owners)
     for y in range(rows_y):
         greeted = greeted + jnp.where(is_owner & (rank(y) < rank(me_y)), 1, 0)
     pl.semaphore_wait(barrier, greeted)
@@ -321,6 +321,13 @@
             device_id=at_group(p), device_id_type=MESH,
         )
 
+    @pl.when(is_owner)
+    def _():
+        ahead = jnp.zeros((1, channels), F32)
+        for m in range(group):
+            decay_s[m] = jnp.exp(ahead)
+            ahead = ahead + totals1[m]
+
     lax.fori_loop(third, middle, inside, 0)
 
     @pl.when(is_owner)
@@ -337,12 +344,11 @@
                 entering_s[...] = state
 
         entering = entering_s[...]
-        ahead = jnp.zeros((1, channels), F32)
-        for m in range(group):
-            back_s[m] = jnp.exp(ahead) * entering + group_prefix[m]
-            ahead = ahead + totals1[m]
         for i in sorted(range(1, group), key=lambda i: i % 2 - 2 * min((i + 1) // 2, (group - i) // 2) - 3 * (i % 2)):
+            p = (me_j + i) % group
+            back_s[p] = decay_s[p] * entering + group_prefix[p]
             copy_e(i).start()
+        back_s[me_j] = decay_s[me_j] * entering + group_prefix[me_j]
         gather3[me_q] = back_s[me_j]
 
     lax.fori_loop(middle, blocks, inside, 0)
@@ -459,7 +465,7 @@
         vmem((group, 1, channels), F32), vmem((group, piece, channels), F32),
         vmem((piece, channels), F32), vmem((1, channels), F32),
         vmem((rows_y, piece, channels), F32), vmem((rows_y, 1, channels), F32),
-        vmem((piece, channels), F32),
+        vmem((piece, channels), F32), vmem((group, 1, channels), F32),
         vmem((group, piece, channels), F32), vmem((owners, piece, channels), F32),
         vmem((tokens, channels), F32),
         vmem((blocks, BLOCK), F32), vmem((nchan, blocks, BLOCK), F32),

time: 27.2 us -> 26.9 us (0.989)
  Pallas kernels: 27.1 us -> 26.7 us
    pallas_call x1, Pallas kernels: 26 us -> 25.6 us  [per_device(): pl.pallas_call(functools.partial(layer, group, rows_y, nchan), out_shape=...]
where the time goes in v6:
time: 26.9 us; the launch traced here: 26.7 us
  Pallas kernels  26.7 us (99%)
    pallas_call x1, Pallas kernels, per_device(): pl.pallas_call(functools.partial(layer, group, rows_y, nchan), out_shape=...  25.6 us
    pallas_call x1, Pallas kernels, per_device(): pl.pallas_call(functools.partial(scale_rows, channels * nchan), out_shape...  1.08 us

profile of v6, /device:TPU:56, one launch (start us, length us, event | category | flops | bytes accessed | tf_op | source)
XLA Modules:
  0.0 26.7 jit_solution(13903925461537122935)
XLA Ops:
  0.0 25.6 %shard_map.82 = (f32[2048,256]{1,0:T(8,128)S(1)}, f32[8,256]{1,0:T(8,128)S(1)}) custom-call(bf16[2048,256]{1,0:T(8,128)(2,1)} %x_hbm.1, bf16[2048,256]{1,0:T(8,128)(2,1)} %gate_hbm.1, bf16[64,2048]{1,0:T(8,128)(2,1)} %bitcast.4, bf16[64,2048]{1,0:T(8,128)(2,1)} %bitcast.5, f32[4,2048]{1,0:T(4,128)} %step_hbm.1, f32[4,2048]{1,0:T(4,128)} %keep_hbm.1, ...), custom_call_target="tpu_custom_call" | custom-call | tf_op jit(solution)/shard_map/pallas_call | solution.py:475
  25.6 1.1 %shard_map.83 = bf16[2048,256]{1,0:T(8,128)(2,1)} custom-call(f32[2048,256]{1,0:T(8,128)S(1)} %get-tuple-element.7.base_ref, f32[8,256]{1,0:T(8,128)S(1)} %get-tuple-element.8.total_ref), custom_call_target="tpu_custom_call" | custom-call | tf_op jit(solution)/shard_map/pallas_call | solution.py:488

commit v7 on v6

--- a/solution.py
+++ b/solution.py
@@ -77,6 +77,11 @@
         lines_of(count, send_sem).wait_send()
 
     owners = group // 2
+    both_lines = nstate * tokens // (2 * channels) + tokens // 2
+
+    def loaded(count, i):
+        ref = lines_s.at[pl.ds(0, count)]
+        pltpu.make_async_copy(ref, ref, load_sem.at[i]).wait()
 
     def rank(y):
         return jnp.minimum(y, rows_y - y) * rows_y + y
@@ -87,16 +92,21 @@
         pltpu.make_async_copy(keep_hbm, keep_step.at[0], keep_sem),
         pltpu.make_async_copy(step_hbm, keep_step.at[1], keep_sem),
         pltpu.make_async_copy(b_hbm, b_s, load_sem.at[0]),
-        pltpu.make_async_copy(x_hbm, x_s, load_sem.at[1]),
+    ]
+    parts = [
+        pltpu.make_async_copy(x_hbm.at[part, :], x_s.at[part, :], load_sem.at[0])
+        for part in (pl.ds(i * (tokens // 4), tokens // 4) for i in range(4))
     ]
     second = [
-        pltpu.make_async_copy(c_hbm, c_s, load_sem.at[2]),
-        pltpu.make_async_copy(gate_hbm, gate_s, load_sem.at[3]),
-        pltpu.make_async_copy(gain_hbm, gain_s, load_sem.at[4]),
+        pltpu.make_async_copy(c_hbm, c_s, load_sem.at[1]),
+        pltpu.make_async_copy(gate_hbm, gate_s, load_sem.at[1]),
+        pltpu.make_async_copy(gain_hbm, gain_s, load_sem.at[1]),
         pltpu.make_async_copy(skip_hbm, skip_s, skip_sem),
     ]
     for copy in first:
         copy.start()
+    for copy in parts:
+        copy.start(priority=1)
 
     barrier = pltpu.get_barrier_semaphore()
 
@@ -147,8 +157,7 @@
     after = dot(k_high, later) + (dot(k_mid, later) + dot(k_low, later))
     coef8[...] = jnp.exp(after) * step8[...]
 
-    first[2].wait()
-    first[3].wait()
+    loaded(both_lines, 0)
     cum8[...] = dot(k_high, upper) + (dot(k_mid, upper) + dot(k_low, upper))
     for k in range(blocks):
         coef = coef8[8 * k : 8 * k + 8, :]
@@ -221,8 +230,8 @@
         prefix_s[k : k + 1, :] = before
         before = before + totals[k : k + 1, :]
 
-    for copy in second:
-        copy.wait()
+    loaded(both_lines + 1, 1)
+    second[-1].wait()
     head_of = lax.broadcasted_iota(jnp.int32, (1, channels), 1) // width
     skip_row = jnp.zeros((1, channels), F32)
     for h in range(heads):
@@ -469,8 +478,8 @@
         vmem((group, piece, channels), F32), vmem((owners, piece, channels), F32),
         vmem((tokens, channels), F32),
         vmem((blocks, BLOCK), F32), vmem((nchan, blocks, BLOCK), F32),
-        vmem(((owners + rows_y) * (piece + 1) + group * piece + nchan * blocks, 1, channels), F32),
-        dma((5,)), dma, dma, pltpu.SemaphoreType.REGULAR((rows_y,)), pltpu.SemaphoreType.REGULAR,
+        vmem((max((owners + rows_y) * (piece + 1) + group * piece + nchan * blocks, nstate * tokens // (2 * channels) + tokens // 2 + 1), 1, channels), F32),
+        dma((2,)), dma, dma, pltpu.SemaphoreType.REGULAR((rows_y,)), pltpu.SemaphoreType.REGULAR,
     ] + [dma] * 5
     base, total = pl.pallas_call(
         functools.partial(layer, group, rows_y, nchan),

time: 26.9 us -> 26.8 us (level)
  no operation moved by 1% of the time
where the time goes in v7:
time: 26.8 us; the launch traced here: 26.6 us
  Pallas kernels  26.6 us (99%)
    pallas_call x1, Pallas kernels, per_device(): pl.pallas_call(functools.partial(layer, group, rows_y, nchan), out_shape=...  25.5 us
    pallas_call x1, Pallas kernels, per_device(): pl.pallas_call(functools.partial(scale_rows, channels * nchan), out_shape...  1.08 us

profile of v7, /device:TPU:56, one launch (start us, length us, event | category | flops | bytes accessed | tf_op | source)
XLA Modules:
  0.0 26.6 jit_solution(10174253841219646341)
XLA Ops:
  0.0 25.5 %shard_map.82 = (f32[2048,256]{1,0:T(8,128)S(1)}, f32[8,256]{1,0:T(8,128)S(1)}) custom-call(bf16[2048,256]{1,0:T(8,128)(2,1)} %x_hbm.1, bf16[2048,256]{1,0:T(8,128)(2,1)} %gate_hbm.1, bf16[64,2048]{1,0:T(8,128)(2,1)} %bitcast.4, bf16[64,2048]{1,0:T(8,128)(2,1)} %bitcast.5, f32[4,2048]{1,0:T(4,128)} %step_hbm.1, f32[4,2048]{1,0:T(4,128)} %keep_hbm.1, ...), custom_call_target="tpu_custom_call" | custom-call | tf_op jit(solution)/shard_map/pallas_call | solution.py:484
  25.5 1.1 %shard_map.83 = bf16[2048,256]{1,0:T(8,128)(2,1)} custom-call(f32[2048,256]{1,0:T(8,128)S(1)} %get-tuple-element.7.base_ref, f32[8,256]{1,0:T(8,128)S(1)} %get-tuple-element.8.total_ref), custom_call_target="tpu_custom_call" | custom-call | tf_op jit(solution)/shard_map/pallas_call | solution.py:497

commit v8 on v7

--- a/solution.py
+++ b/solution.py
@@ -187,6 +187,12 @@
         greeted = greeted + jnp.where(is_owner & (rank(y) < rank(me_y)), 1, 0)
     pl.semaphore_wait(barrier, greeted)
 
+    for y in range(rows_y):
+
+        @pl.when(is_owner & (y < me_y) & (rank(y) < rank(me_y)))
+        def _():
+            report(y_in.at[me_y], at_y(y))
+
     def copy_a(i):
         return pltpu.make_async_remote_copy(
             device_total, totals1.at[me_j], send_sem, b_recv,
@@ -207,12 +213,6 @@
         def _():
             copy_a(i).start()
             copy_b(i).start()
-
-    for y in range(rows_y):
-
-        @pl.when(is_owner & (y < me_y) & (rank(y) < rank(me_y)))
-        def _():
-            report(y_in.at[me_y], at_y(y))
 
     for z in range(nchan):
 

time: 26.8 us -> 26.8 us (level)
  no operation moved by 1% of the time
where the time goes in v8:
time: 26.8 us; the launch traced here: 26.7 us
  Pallas kernels  26.7 us (100%)
    pallas_call x1, Pallas kernels, per_device(): pl.pallas_call(functools.partial(layer, group, rows_y, nchan), out_shape=...  25.6 us
    pallas_call x1, Pallas kernels, per_device(): pl.pallas_call(functools.partial(scale_rows, channels * nchan), out_shape...  1.08 us

profile of v8, /device:TPU:56, one launch (start us, length us, event | category | flops | bytes accessed | tf_op | source)
XLA Modules:
  0.0 26.7 jit_solution(6924020301806805814)
XLA Ops:
  0.0 25.6 %shard_map.82 = (f32[2048,256]{1,0:T(8,128)S(1)}, f32[8,256]{1,0:T(8,128)S(1)}) custom-call(bf16[2048,256]{1,0:T(8,128)(2,1)} %x_hbm.1, bf16[2048,256]{1,0:T(8,128)(2,1)} %gate_hbm.1, bf16[64,2048]{1,0:T(8,128)(2,1)} %bitcast.4, bf16[64,2048]{1,0:T(8,128)(2,1)} %bitcast.5, f32[4,2048]{1,0:T(4,128)} %step_hbm.1, f32[4,2048]{1,0:T(4,128)} %keep_hbm.1, ...), custom_call_target="tpu_custom_call" | custom-call | tf_op jit(solution)/shard_map/pallas_call | solution.py:484
  25.6 1.1 %shard_map.83 = bf16[2048,256]{1,0:T(8,128)(2,1)} custom-call(f32[2048,256]{1,0:T(8,128)S(1)} %get-tuple-element.7.base_ref, f32[8,256]{1,0:T(8,128)S(1)} %get-tuple-element.8.total_ref), custom_call_target="tpu_custom_call" | custom-call | tf_op jit(solution)/shard_map/pallas_call | solution.py:497
